TPU v7x, 512 devices: a whole 4x4x16 slice. The times are simulated.
512 devices in a mesh: ta: 4 (over x), xy: 16 (over z), gz: 8 (over y, core).
Axes of the slice: x: 4, y: 4, z: 16, core: 2. Of those that a mesh axis runs over, the one named last changes fastest.
Arguments:
- propagator: float32 [2, 4, 4, 9, 128, 16384], P(None, None, None, None, 'ta', ('xy', 'gz')), as said below
- site_coords: int32 [3, 16384], P(None, ('xy', 'gz')), may hold values from 0 to 95
- momenta: int32 [3, 64], replicated, may hold values from 1 to 4
- source_slice: int32 [4], replicated, may hold values from 0 to 127
Outputs:
- correlator: float32 [16, 128, 128], P(None, 'ta')
Inputs may be any that keep to these rules, and one draw needn't show every extreme that they name: `momenta`: each component of a momentum lies in 1 to 4. `site_coords`: each site coordinate. `propagator`: real-valued entries of order one, with a scale that differs between time slices.
All inputs are finite; a program needn't handle non-finite values.
Results may differ from a plain program's by a relative error of at most 0.000071.
Values sent between devices are 32-bit elements; how exact they have to be, the bound alone decides.
No kernel may reach another device: no remote copies, remote signals or barrier semaphores. Data moves between devices by JAX's collectives and lax.ppermute only.
A program may use at most 64 MiB of HBM per device.

v0:
```python
import functools
import math

import jax
import jax.numpy as jnp
from jax import lax
from jax.sharding import Mesh
from jax.sharding import PartitionSpec as P

EXTENT = 96
XY_GZ = ("xy", "gz_0", "gz_1")
GZ = ("gz_0", "gz_1")


def one_axis_at_a_time(x, axes):
    return functools.reduce(lax.psum, axes, x)


def sent_to_all(x, axis):
    copies = jnp.broadcast_to(x, (lax.axis_size(axis), *x.shape))
    return lax.all_to_all(copies, axis, split_axis=0, concat_axis=0, tiled=True)


def over_copies(x, axis):
    everything = sent_to_all(x, axis)
    return jnp.sum(everything, axis=0)


def split_up(x, dim, devices):
    lengths = x.shape
    pieces = x.reshape(*lengths[:dim], devices, lengths[dim] // devices, *lengths[dim + 1 :])
    return jnp.moveaxis(pieces, dim, 0)


def sum_at_owner(x, axis, dim):
    devices = lax.axis_size(axis)
    pieces = lax.all_to_all(split_up(x, dim, devices), axis, 0, 0, tiled=True)
    return jnp.sum(pieces, axis=0)


def gathered_total(x, axis):
    return lax.all_gather(x, axis).sum(0)


def in_order(pieces, dim):
    lengths = list(pieces.shape[1:])
    lengths[dim] *= pieces.shape[0]
    return jnp.moveaxis(pieces, 0, dim).reshape(lengths)


def collect(x, axis, dim):
    pieces = sent_to_all(x, axis)
    return in_order(pieces, dim)


def phase_table(site_coords, momenta):
    turns = jnp.dot(site_coords.T, momenta)
    turns = jnp.remainder(turns, EXTENT)
    angles = turns.astype(jnp.float32) * jnp.float32(2.0 * math.pi / EXTENT)
    return jnp.concatenate([jnp.cos(angles), -jnp.sin(angles)], axis=1)


def on_device(propagator, site_coords, momenta, source_slice):
    slices = propagator.shape[4]
    local_sites = propagator.shape[5]
    pairs = propagator.shape[1] * propagator.shape[2]
    phases = phase_table(site_coords, momenta)
    density = jnp.sum(jnp.square(propagator), axis=(0, 3)).reshape(pairs * slices, local_sites)
    partial_value = jnp.dot(
        density, phases, precision=lax.Precision.HIGHEST, preferred_element_type=jnp.float32
    )
    slice_total = jnp.sum(density.reshape(pairs, slices, local_sites), axis=(0, 2))
    offset = lax.axis_index("ta") * slices
    picked = jnp.arange(slices, dtype=jnp.int32)[:, None] + offset == source_slice[None, :]
    counts = jnp.sum(picked.astype(jnp.float32), axis=1)
    plane_total = one_axis_at_a_time(slice_total, XY_GZ)
    grand_total = over_copies(jnp.sum(counts * plane_total), "ta")
    share_rows = sum_at_owner(partial_value, GZ, 0)
    share_rows = gathered_total(share_rows, "xy")
    summed = collect(share_rows, GZ, 0)
    all_sites = jnp.float32(local_sites * lax.axis_size("xy") * lax.axis_size(GZ))
    grand_total = jnp.maximum(grand_total, all_sites)
    slice_norm = jnp.maximum(plane_total, all_sites)
    correlator = (
        summed.reshape(pairs, slices, phases.shape[1])
        * jnp.sqrt(grand_total)
        / slice_norm[None, :, None]
    )
    return correlator


def solution(mesh):
    finer = Mesh(
        mesh.devices.reshape(mesh.shape["ta"], mesh.shape["xy"], 4, 2), ("ta", "xy", "gz_0", "gz_1")
    )
    return jax.shard_map(
        on_device,
        mesh=finer,
        in_specs=(P(None, None, None, None, "ta", XY_GZ), P(None, XY_GZ), P(), P()),
        out_specs=P(None, "ta", None),
        check_vma=False,
    )
```

profile of v0, /device:TPU:1, one launch (start us, length us, event | category | flops | bytes accessed | tf_op | source)
XLA Modules:
  0.0 107.1 jit_solution(14494035872097277057)
XLA Ops:
  0.0 0.0 copy-start
  0.0 0.0 copy-start.1
  0.0 0.0 copy-start.2
  0.0 3.1 %multiply_reduce_fusion = (f32[32]{0:T(128)S(1)}, f32[4,4,32,128]{3,2,1,0:T(8,128)S(1)}) fusion(f32[2,4,4,9,32,128]{5,4,3,2,1,0:T(8,128)} %param.4), kind=kLoop, calls=%fused_computation | loop fusion | flops 3473376 | bytes 4980864 | tf_op jit(solution)/shard_map/reduce_sum | solution.py:72
  3.2 0.0 copy-done
  3.2 0.0 copy-done.1
  3.2 0.4 fusion.6
  3.6 1.1 %fusion = f32[8,64,128]{2,1,0:T(8,128)} fusion(f32[8,64,128]{2,1,0:T(8,128)S(1)} %bitcast.10, f32[128,64]{0,1:T(8,128)S(1)} %get-tuple-element.8, f32[128,64]{0,1:T(8,128)S(1)} %get-tuple-element.7), kind=kOutput, calls=%fused_computation.6 | convolution fusion | flops 100679680 | bytes 589824 | tf_op jit(solution)/shard_map/dot_general | solution.py:69
  4.7 10.2 %all-to-all-start = ((f32[8,64,128]{2,1,0:T(8,128)}), f32[8,64,128]{2,1,0:T(8,128)S(1)}, u32[]{:S(2)}, u32[]{:S(2)}) async-start(f32[8,64,128]{2,1,0:T(8,128)} %fusion), calls=%async_computation | async-start | bytes 524288 | tf_op jit(solution)/shard_map/all_to_all | solution.py:37
  14.8 0.0 copy-done.2
  14.8 0.1 convert_reduce_fusion
  14.9 25.5 %psum.21 = f32[32]{0:T(128)S(1)} all-reduce(f32[32]{0:T(128)S(1)} %get-tuple-element.5), channel_id=1, replica_groups=mesh['ta'=4,'xy'=16,'gz_0'=4,'gz_1'=2] {'xy'}, use_global_device_ids=true, to_apply=%region_5.6 | all-reduce | flops 32 | bytes 256 | tf_op jit(solution)/shard_map/psum | solution.py:16
  40.4 8.4 %psum.22 = f32[32]{0:T(128)S(1)} all-reduce(f32[32]{0:T(128)S(1)} %psum.21), channel_id=1, replica_groups=mesh['ta'=4,'xy'=16,'gz_0'=4,'gz_1'=2] {'gz_0'}, use_global_device_ids=true, to_apply=%region_6.7 | all-reduce | flops 32 | bytes 256 | tf_op jit(solution)/shard_map/psum | solution.py:16
  48.8 11.5 %psum.23 = f32[32]{0:T(128)S(1)} all-reduce(f32[32]{0:T(128)S(1)} %psum.22), channel_id=1, replica_groups=mesh['ta'=4,'xy'=16,'gz_0'=4,'gz_1'=2] {'gz_1'}, use_global_device_ids=true, to_apply=%region_7.8 | all-reduce | flops 32 | bytes 256 | tf_op jit(solution)/shard_map/psum | solution.py:16
  60.3 0.7 broadcast_maximum_fusion
  61.0 0.0 all-to-all-done
  61.0 1.3 %broadcast_in_dim.10 = f32[4,1,1]{2,1,0:T(1,128)} broadcast(f32[]{:T(128)} %get-tuple-element.10), dimensions={} | broadcast | bytes 20 | tf_op jit(solution)/shard_map/broadcast_in_dim | solution.py:20
  62.3 4.0 %all-to-all-start.2 = ((f32[4,1,1]{2,1,0:T(1,128)}), f32[4,1,1]{2,1,0:T(1,128)S(1)}, u32[]{:S(2)}, u32[]{:S(2)}) async-start(f32[4,1,1]{2,1,0:T(1,128)} %broadcast_in_dim.10), calls=%async_computation.2 | async-start | bytes 4096 | tf_op jit(solution)/shard_map/all_to_all | solution.py:21
  66.3 22.0 %all-gather = f32[1024,128]{1,0:T(8,128)S(1)} all-gather(f32[64,128]{1,0:T(8,128)S(1)} %reduce_sum.64), channel_id=2, replica_groups=mesh['ta'=4,'xy'=16,'gz_0'=4,'gz_1'=2] {'xy'}, dimensions={0}, use_global_device_ids=true | all-gather | bytes 557056 | tf_op jit(solution)/shard_map/all_gather | solution.py:42
  88.4 0.0 all-to-all-done.2
  88.4 0.7 broadcast_in_dim.4
  89.1 10.7 %all-to-all-start.1 = ((f32[8,64,128]{2,1,0:T(8,128)}), f32[8,64,128]{2,1,0:T(8,128)S(1)}, u32[]{:S(2)}, u32[]{:S(2)}) async-start(f32[8,64,128]{2,1,0:T(8,128)} %broadcast_in_dim.4), calls=%async_computation.1 | async-start | bytes 524288 | tf_op jit(solution)/shard_map/all_to_all | solution.py:21
  99.8 0.7 reduce_sum.69
  101.2 5.1 %all-to-all-done.1 = f32[8,64,128]{2,1,0:T(8,128)S(1)} async-done(((f32[8,64,128]{2,1,0:T(8,128)}), f32[8,64,128]{2,1,0:T(8,128)S(1)}, u32[]{:S(2)}, u32[]{:S(2)}) %all-to-all-start.1) | async-done | bytes 262176 | tf_op jit(solution)/shard_map/all_to_all | solution.py:21
  106.3 0.8 broadcast_divide_fusion
  (4 shorter events, 0.1 us)
Async XLA Ops:
  0.0 3.2 %copy-start = (s32[3,128]{1,0:T(4,128)S(1)}, s32[3,128]{1,0:T(4,128)}, u32[]{:S(2)}) copy-start(s32[3,128]{1,0:T(4,128)} %param.5) | copy-start | bytes 4612
  0.0 3.2 %copy-start.1 = (s32[3,64]{1,0:T(4,128)S(1)}, s32[3,64]{1,0:T(4,128)}, u32[]{:S(2)}) copy-start(s32[3,64]{1,0:T(4,128)} %param.6) | copy-start | bytes 2308
  0.0 14.8 %copy-start.2 = (s32[4]{0:T(128)S(1)}, s32[4]{0:T(128)}, u32[]{:S(2)}) copy-start(s32[4]{0:T(128)} %param.7) | copy-start | bytes 52
  4.7 56.3 %all-to-all-start = ((f32[8,64,128]{2,1,0:T(8,128)}), f32[8,64,128]{2,1,0:T(8,128)S(1)}, u32[]{:S(2)}, u32[]{:S(2)}) async-start(f32[8,64,128]{2,1,0:T(8,128)} %fusion), calls=%async_computation | async-start | bytes 524288 | tf_op jit(solution)/shard_map/all_to_all | solution.py:37
  62.3 26.1 %all-to-all-start.2 = ((f32[4,1,1]{2,1,0:T(1,128)}), f32[4,1,1]{2,1,0:T(1,128)S(1)}, u32[]{:S(2)}, u32[]{:S(2)}) async-start(f32[4,1,1]{2,1,0:T(1,128)} %broadcast_in_dim.10), calls=%async_computation.2 | async-start | bytes 4096 | tf_op jit(solution)/shard_map/all_to_all | solution.py:21
  89.1 17.2 %all-to-all-start.1 = ((f32[8,64,128]{2,1,0:T(8,128)}), f32[8,64,128]{2,1,0:T(8,128)S(1)}, u32[]{:S(2)}, u32[]{:S(2)}) async-start(f32[8,64,128]{2,1,0:T(8,128)} %broadcast_in_dim.4), calls=%async_computation.1 | async-start | bytes 524288 | tf_op jit(solution)/shard_map/all_to_all | solution.py:21
where the time goes:
time: 108 us; the launch traced here: 107 us
  blocking collectives  67.4 us (62%)
  starting transfers between devices  24.8 us (23%)
  other arithmetic  5.48 us (5%)
  waiting for transfers between devices  5.08 us (5%)
  local copies, waits for them, and re-layouts  2 us (2%)
  matrix products  1.5 us (1%)
    psum x3, blocking collectives, one_axis_at_a_time(): return functools.reduce(lax.psum, axes, x)  45.4 us
    all_gather x1, blocking collectives, gathered_total(): return lax.all_gather(x, axis).sum(0)  22 us
    all_to_all x2, starting transfers between devices, sent_to_all(): return lax.all_to_all(copies, axis, split_axis=0, concat_axis=0, tiled=True)  14.7 us
    all_to_all x1, starting transfers between devices, sum_at_owner(): pieces = lax.all_to_all(split_up(x, dim, devices), axis, 0, 0, tiled=True)  10.2 us
    all_to_all x2, waiting for transfers between devices, sent_to_all(): return lax.all_to_all(copies, axis, split_axis=0, concat_axis=0, tiled=True)  5.08 us
    reduce_sum x1, other arithmetic, on_device(): jnp.sum(density.reshape(pairs, slices, local_sites), axis=(0, 2))  3.15 us
  transfers between devices with their start and end apart: 3, of which 1 were waited for; matrix products, arithmetic and copies ran while one was open for 1% of the time, Pallas kernels for 0%

commit v1 on v0

v1 whole, which is shorter than its diff:
```python
import math

import jax
import jax.numpy as jnp
from jax import lax
from jax.sharding import Mesh
from jax.sharding import PartitionSpec as P

EXTENT = 96
GZ = ("gz_0", "gz_1")
NEAR = ("z_lo", "gz_0", "gz_1")
FAR = "z_hi"
SITE_AXES = ("z_hi", "z_lo", "gz_0", "gz_1")


def exchange(x, axes):
    return lax.all_to_all(x, axes, split_axis=0, concat_axis=0, tiled=True)


def copies(x, axes):
    return jnp.broadcast_to(x, (lax.axis_size(axes), *x.shape))


def phase_table(site_coords, momenta):
    turns = jnp.dot(site_coords.T, momenta)
    turns = jnp.remainder(turns, EXTENT)
    angles = turns.astype(jnp.float32) * jnp.float32(2.0 * math.pi / EXTENT)
    return jnp.concatenate([jnp.cos(angles), -jnp.sin(angles)], axis=1)


def on_device(propagator, site_coords, momenta, source_slice):
    slices = propagator.shape[4]
    local_sites = propagator.shape[5]
    pairs = propagator.shape[1] * propagator.shape[2]
    near = lax.axis_size(NEAR)
    rows = pairs * slices // near
    phases = phase_table(site_coords, momenta)
    density = jnp.sum(jnp.square(propagator), axis=(0, 3)).reshape(pairs * slices, local_sites)
    partial_value = jnp.dot(
        density, phases, precision=lax.Precision.HIGHEST, preferred_element_type=jnp.float32
    )
    lanes = partial_value.shape[1]
    slice_total = jnp.sum(density.reshape(pairs, slices, local_sites), axis=(0, 2))
    stats = jnp.pad(slice_total, (0, lanes - slices))

    blocks = partial_value.reshape(near, rows, 1, lanes)
    blocks = jnp.concatenate([blocks, copies(stats[None, None, :], NEAR)], axis=1)
    near_sum = jnp.sum(exchange(blocks, NEAR), axis=0)
    far_sum = jnp.sum(exchange(copies(near_sum, FAR), FAR), axis=0)

    plane_total = far_sum[rows, 0, :slices]
    offset = lax.axis_index("ta") * slices
    picked = jnp.arange(slices, dtype=jnp.int32)[:, None] + offset == source_slice[None, :]
    counts = jnp.sum(picked.astype(jnp.float32), axis=1)
    mine = jnp.broadcast_to(jnp.sum(counts * plane_total), (1, lanes))
    grand_total = jnp.sum(exchange(copies(mine, "ta"), "ta")[:, 0, 0])

    all_sites = jnp.float32(local_sites * lax.axis_size(SITE_AXES))
    scaled = far_sum[:rows, 0, :].reshape(rows // slices, slices, lanes)
    scaled = scaled / jnp.maximum(plane_total, all_sites)[None, :, None]
    gathered = exchange(copies(scaled.reshape(rows, lanes), NEAR), NEAR)
    correlator = gathered * jnp.sqrt(jnp.maximum(grand_total, all_sites))
    return correlator.reshape(pairs, slices, lanes)


def solution(mesh):
    finer = Mesh(
        mesh.devices.reshape(mesh.shape["ta"], mesh.shape["xy"] // 2, 2, 4, 2),
        ("ta", "z_hi", "z_lo", "gz_0", "gz_1"),
    )
    return jax.shard_map(
        on_device,
        mesh=finer,
        in_specs=(P(None, None, None, None, "ta", SITE_AXES), P(None, SITE_AXES), P(), P()),
        out_specs=P(None, "ta", None),
        check_vma=False,
    )
```

time: 108 us -> 74.6 us (0.69)
  blocking collectives: 67.4 us -> 16.6 us
  waiting for transfers between devices: 5.08 us -> 22.9 us
    psum x3 -> x0, blocking collectives: 45.4 us -> none  [one_axis_at_a_time(): return functools.reduce(lax.psum, axes, x)]
    all_gather x1 -> x0, blocking collectives: 22 us -> none  [gathered_total(): return lax.all_gather(x, axis).sum(0)]
    all_to_all x3, waiting for transfers between devices: 5.08 us -> 22.9 us  [exchange(): return lax.all_to_all(x, axes, split_axis=0, concat_axis=0, tiled=True)]
    all_to_all x0 -> x1, blocking collectives: none -> 16.6 us  [exchange(): return lax.all_to_all(x, axes, split_axis=0, concat_axis=0, tiled=True)]
    another operation x0 -> x1, local copies, waits for them, and re-layouts: none -> 1.27 us  [copies(): return jnp.broadcast_to(x, (lax.axis_size(axes), *x.shape))]
    reduce_sum x4 -> x5, other arithmetic: 3.88 us -> 4.8 us  [the longest x1 3.16 us: on_device(): jnp.sum(jnp.square(propagator), axis=(0, 3))]
  transfers between devices with their start and end apart: 3 -> 3, of which waited for: 1 -> 3; matrix products, arithmetic and copies ran while one was open for 1% -> 1% of each run, Pallas kernels for 0% -> 0%
where the time goes in v1:
time: 74.6 us; the launch traced here: 74.2 us
  starting transfers between devices  24.4 us (33%)
  waiting for transfers between devices  22.9 us (31%)
  blocking collectives  16.6 us (22%)
  other arithmetic  5.71 us (8%)
  local copies, waits for them, and re-layouts  3.02 us (4%)
  between operations  0.82 us (1%)
  matrix products  0.79 us (1%)
    all_to_all x3, starting transfers between devices, exchange(): return lax.all_to_all(x, axes, split_axis=0, concat_axis=0, tiled=True)  24.4 us
    all_to_all x3, waiting for transfers between devices, exchange(): return lax.all_to_all(x, axes, split_axis=0, concat_axis=0, tiled=True)  22.9 us
    all_to_all x1, blocking collectives, exchange(): return lax.all_to_all(x, axes, split_axis=0, concat_axis=0, tiled=True)  16.6 us
    reduce_sum x1, other arithmetic, on_device(): jnp.sum(jnp.square(propagator), axis=(0, 3))  3.16 us
  transfers between devices with their start and end apart: 3, of which 3 were waited for; matrix products, arithmetic and copies ran while one was open for 1% of the time, Pallas kernels for 0%

profile of v1, /device:TPU:1, one launch (start us, length us, event | category | flops | bytes accessed | tf_op | source)
XLA Modules:
  0.0 74.2 jit_solution(14324304607361528650)
XLA Ops:
  0.0 0.0 copy-start
  0.0 0.0 copy-start.1
  0.0 0.0 copy-start.2
  0.0 3.2 %multiply_reduce_fusion.1 = (f32[4,4,32,128]{3,2,1,0:T(8,128)S(1)}, f32[32]{0:T(128)S(1)}) fusion(f32[2,4,4,9,32,128]{5,4,3,2,1,0:T(8,128)} %param.4), kind=kLoop, calls=%fused_computation.1 | loop fusion | flops 3473376 | bytes 4980864 | tf_op jit(solution)/shard_map/reduce_sum | solution.py:38
  3.2 0.0 copy-done
  3.2 0.0 copy-done.1
  3.2 0.4 fusion.6
  3.6 0.4 convolution_bitcast_fusion
  4.0 0.3 copy.11
  4.3 16.6 %all_to_all.20 = f32[16,33,1,128]{3,2,1,0:T(1,128)S(1)} all-to-all(f32[16,33,1,128]{3,2,1,0:T(1,128)S(1)} %copy.11), channel_id=1, replica_groups=mesh['ta'=4,'z_hi'=8,'z_lo'=2,'gz_0'=4,'gz_1'=2] {'z_lo','gz_0','gz_1'}, dimensions={0} | all-to-all | bytes 540672 | tf_op jit(solution)/shard_map/all_to_all | solution.py:17
  20.9 0.2 reduce_sum.67
  21.1 0.7 broadcast_in_dim.14
  21.8 11.7 %all-to-all-start.1 = ((f32[8,33,1,128]{3,2,1,0:T(1,128)}), f32[8,33,1,128]{3,2,1,0:T(1,128)S(1)}, u32[]{:S(2)}, u32[]{:S(2)}) async-start(f32[8,33,1,128]{3,2,1,0:T(1,128)} %broadcast_in_dim.14), calls=%async_computation.1 | async-start | bytes 270336 | tf_op jit(solution)/shard_map/all_to_all | solution.py:17
  33.5 0.0 copy-done.2
  33.6 0.1 convert_reduce_fusion
  33.6 13.1 %all-to-all-done.1 = f32[8,33,1,128]{3,2,1,0:T(1,128)S(1)} async-done(((f32[8,33,1,128]{3,2,1,0:T(1,128)}), f32[8,33,1,128]{3,2,1,0:T(1,128)S(1)}, u32[]{:S(2)}, u32[]{:S(2)}) %all-to-all-start.1) | async-done | bytes 135200 | tf_op jit(solution)/shard_map/all_to_all | solution.py:17
  46.7 0.1 reduce_sum.68
  46.8 0.7 multiply_reduce_fusion.2
  47.5 1.3 %broadcast_in_dim_broadcast_in_dim.3 = f32[4,1,128]{2,1,0:T(1,128)} broadcast(f32[]{:T(128)} %get-tuple-element.9), dimensions={} | broadcast | bytes 2052 | tf_op jit(solution)/shard_map/broadcast_in_dim;broadcast_in_dim | solution.py:21
  48.8 4.0 %all-to-all-start.3 = ((f32[4,1,128]{2,1,0:T(1,128)}), f32[4,1,128]{2,1,0:T(1,128)S(1)}, u32[]{:S(2)}, u32[]{:S(2)}) async-start(f32[4,1,128]{2,1,0:T(1,128)} %broadcast_in_dim_broadcast_in_dim.3), calls=%async_computation.3 | async-start | bytes 4096 | tf_op jit(solution)/shard_map/all_to_all | solution.py:17
  52.8 0.1 slice_divide_fusion
  52.9 4.0 %all-to-all-done.3 = f32[4,1,128]{2,1,0:T(1,128)S(1)} async-done(((f32[4,1,128]{2,1,0:T(1,128)}), f32[4,1,128]{2,1,0:T(1,128)S(1)}, u32[]{:S(2)}, u32[]{:S(2)}) %all-to-all-start.3) | async-done | bytes 2080 | tf_op jit(solution)/shard_map/all_to_all | solution.py:17
  56.9 0.7 broadcast_in_dim.15
  57.6 8.7 %all-to-all-start.2 = ((f32[16,32,128]{2,1,0:T(8,128)}), f32[16,32,128]{2,1,0:T(8,128)S(1)}, u32[]{:S(2)}, u32[]{:S(2)}) async-start(f32[16,32,128]{2,1,0:T(8,128)} %broadcast_in_dim.15), calls=%async_computation.2 | async-start | bytes 524288 | tf_op jit(solution)/shard_map/all_to_all | solution.py:17
  66.3 0.7 slice_reduce_fusion
  67.7 5.8 %all-to-all-done.2 = f32[16,32,128]{2,1,0:T(8,128)S(1)} async-done(((f32[16,32,128]{2,1,0:T(8,128)}), f32[16,32,128]{2,1,0:T(8,128)S(1)}, u32[]{:S(2)}, u32[]{:S(2)}) %all-to-all-start.2) | async-done | bytes 262176 | tf_op jit(solution)/shard_map/all_to_all | solution.py:17
  73.5 0.7 broadcast_multiply_fusion
  (4 shorter events, 0.0 us)
Async XLA Ops:
  0.0 3.2 %copy-start = (s32[3,128]{1,0:T(4,128)S(1)}, s32[3,128]{1,0:T(4,128)}, u32[]{:S(2)}) copy-start(s32[3,128]{1,0:T(4,128)} %param.5) | copy-start | bytes 4612
  0.0 3.2 %copy-start.1 = (s32[3,64]{1,0:T(4,128)S(1)}, s32[3,64]{1,0:T(4,128)}, u32[]{:S(2)}) copy-start(s32[3,64]{1,0:T(4,128)} %param.6) | copy-start | bytes 2308
  0.0 33.5 %copy-start.2 = (s32[4]{0:T(128)S(1)}, s32[4]{0:T(128)}, u32[]{:S(2)}) copy-start(s32[4]{0:T(128)} %param.7) | copy-start | bytes 52
  21.8 24.9 %all-to-all-start.1 = ((f32[8,33,1,128]{3,2,1,0:T(1,128)}), f32[8,33,1,128]{3,2,1,0:T(1,128)S(1)}, u32[]{:S(2)}, u32[]{:S(2)}) async-start(f32[8,33,1,128]{3,2,1,0:T(1,128)} %broadcast_in_dim.14), calls=%async_computation.1 | async-start | bytes 270336 | tf_op jit(solution)/shard_map/all_to_all | solution.py:17
  48.8 8.1 %all-to-all-start.3 = ((f32[4,1,128]{2,1,0:T(1,128)}), f32[4,1,128]{2,1,0:T(1,128)S(1)}, u32[]{:S(2)}, u32[]{:S(2)}) async-start(f32[4,1,128]{2,1,0:T(1,128)} %broadcast_in_dim_broadcast_in_dim.3), calls=%async_computation.3 | async-start | bytes 4096 | tf_op jit(solution)/shard_map/all_to_all | solution.py:17
  57.6 15.9 %all-to-all-start.2 = ((f32[16,32,128]{2,1,0:T(8,128)}), f32[16,32,128]{2,1,0:T(8,128)S(1)}, u32[]{:S(2)}, u32[]{:S(2)}) async-start(f32[16,32,128]{2,1,0:T(8,128)} %broadcast_in_dim.15), calls=%async_computation.2 | async-start | bytes 524288 | tf_op jit(solution)/shard_map/all_to_all | solution.py:17

commit v2 on v1

v2 whole, which is shorter than its diff:
```python
import functools
import math

import jax
import jax.numpy as jnp
from jax import lax
from jax.experimental import pallas as pl
from jax.experimental.pallas import tpu as pltpu
from jax.sharding import PartitionSpec as P

EXTENT = 96
SITE_AXES = ("xy", "gz")
IN_HBM = pl.BlockSpec(memory_space=pltpu.HBM)
IN_VMEM = pl.BlockSpec(memory_space=pltpu.VMEM)


def plane(pair, member, pairs):
    return 2 * pair + (member if 2 * pair < pairs else 1 - member)


def groups(planes, blocks):
    pairs = planes // 2
    near = [
        [plane(p, m, pairs) * blocks + g for m in range(2) for g in range(blocks)]
        for p in range(pairs)
    ]
    far = [[plane(p, m, pairs) for p in range(pairs)] for m in range(2)]
    return near, far


def exchange(x, axes, axis_groups=None):
    return lax.all_to_all(
        x, axes, split_axis=0, concat_axis=0, tiled=True, axis_index_groups=axis_groups
    )


def phase_table(coords, momenta):
    both = jnp.concatenate([momenta, momenta], axis=1)
    turns = lax.dot_general(
        coords, both, (((0,), (0,)), ((), ())), preferred_element_type=jnp.float32
    )
    lane = lax.broadcasted_iota(jnp.int32, turns.shape, 1)
    turns = turns + jnp.where(lane >= momenta.shape[1], EXTENT / 4.0, 0.0)
    turns = turns - EXTENT * jnp.floor((turns + 0.5) * (1.0 / EXTENT))
    angle = (jnp.abs(turns - EXTENT / 2.0) - EXTENT / 4.0) * (2.0 * math.pi / EXTENT)
    square = angle * angle
    series = jnp.full_like(square, 1.0 / math.factorial(13))
    for power in (11, 9, 7, 5, 3, 1):
        sign = -1.0 if power % 4 == 3 else 1.0
        series = series * square + sign / math.factorial(power)
    return series * angle


def project_kernel(
    near, propagator, coords, momenta, source, out, parts, site_buf, mom_buf, src_buf, density,
    total, part_sem, small_sem,
):
    _, sinks, sources, colors, slices, _ = propagator.shape
    pairs = sinks * sources
    lanes = out.shape[1]
    rows = pairs * slices // near
    loads = [
        pltpu.make_async_copy(coords, site_buf, small_sem.at[0]),
        pltpu.make_async_copy(momenta, mom_buf, small_sem.at[1]),
        pltpu.make_async_copy(source, src_buf, small_sem.at[2]),
    ]
    for load in loads:
        load.start()
    copies = [
        pltpu.make_async_copy(
            propagator.at[:, p // sources, p % sources], parts.at[p], part_sem.at[p]
        )
        for p in range(pairs)
    ]
    for copy in copies:
        copy.start()
    for load in loads:
        load.wait()
    phases = phase_table(site_buf[...].astype(jnp.float32), mom_buf[...].astype(jnp.float32))
    first = lax.axis_index("ta") * slices
    lane = lax.broadcasted_iota(jnp.int32, (8, lanes), 1)
    counts = jnp.zeros((8, lanes), jnp.float32)
    for i in range(source.shape[0]):
        counts = counts + jnp.where(lane == src_buf[i] - first, 1.0, 0.0)
    total[...] = jnp.zeros_like(total)
    step = 4
    over_pairs = None
    for p in range(pairs):
        copies[p].wait()
        value = None
        for r in range(2):
            for c in range(colors):
                part = parts[p, r, c]
                value = part * part if value is None else value + part * part
        density[p * slices : (p + 1) * slices] = value
        over_pairs = value if over_pairs is None else over_pairs + value
        if p % step == step - 1:
            begin = (p + 1 - step) * slices
            projected = jnp.dot(
                density[begin : begin + step * slices],
                phases,
                precision=lax.Precision.HIGHEST,
                preferred_element_type=jnp.float32,
            )
            for part in range(step * slices // rows):
                block = begin // rows + part
                out[block * (rows + 1) : block * (rows + 1) + rows] = projected[
                    part * rows : (part + 1) * rows
                ]
    total[:slices] = over_pairs
    by_slice = lax.dot_general(
        jnp.ones((8, total.shape[1]), jnp.float32),
        total[...],
        (((1,), (1,)), ((), ())),
        precision=lax.Precision.HIGHEST,
        preferred_element_type=jnp.float32,
    )
    picked = jnp.sum(by_slice * counts, axis=1, keepdims=True)
    stats = jnp.where(lane < slices, by_slice, picked)
    for block in range(near):
        out[block * (rows + 1) + rows : (block + 1) * (rows + 1)] = stats[:1]


def project(propagator, coords, momenta, source, near):
    _, sinks, sources, colors, slices, sites = propagator.shape
    pairs = sinks * sources
    lanes = 2 * momenta.shape[1]
    return pl.pallas_call(
        functools.partial(project_kernel, near),
        out_shape=jax.ShapeDtypeStruct((pairs * slices + near, lanes), jnp.float32),
        in_specs=[IN_HBM] * 4,
        out_specs=IN_VMEM,
        scratch_shapes=[
            pltpu.VMEM((pairs, 2, colors, slices, sites), jnp.float32),
            pltpu.VMEM(coords.shape, jnp.int32),
            pltpu.VMEM(momenta.shape, jnp.int32),
            pltpu.SMEM(source.shape, jnp.int32),
            pltpu.VMEM((pairs * slices, sites), jnp.float32),
            pltpu.VMEM((lanes, sites), jnp.float32),
            pltpu.SemaphoreType.DMA((pairs,)),
            pltpu.SemaphoreType.DMA((3,)),
        ],
        compiler_params=pltpu.CompilerParams(vmem_limit_bytes=12 << 20),
    )(*[pltpu.with_memory_space_constraint(x, pltpu.HBM) for x in (propagator, coords, momenta, source)])


def sum_of_blocks(ref, blocks):
    rows = ref.shape[0] // blocks
    value = ref[:rows]
    for b in range(1, blocks):
        value = value + ref[b * rows : (b + 1) * rows]
    return value


def near_kernel(near, far, received, out):
    value = sum_of_blocks(received, near)
    rows = value.shape[0]
    for b in range(far):
        out[b * rows : (b + 1) * rows] = value


def far_kernel(far, slices, floor, received, out, picked):
    value = sum_of_blocks(received, far)
    rows = value.shape[0] - 1
    lanes = value.shape[1]
    stats = value[rows:]
    row = lax.broadcasted_iota(jnp.int32, (slices, lanes), 0)
    lane = lax.broadcasted_iota(jnp.int32, (slices, lanes), 1)
    column = jnp.sum(jnp.where(row == lane, stats, 0.0), axis=1, keepdims=True)
    norm = jnp.maximum(column, floor)
    for pair in range(rows // slices):
        scaled = value[pair * slices : (pair + 1) * slices] / norm
        for b in range(out.shape[0]):
            out[b, pair * slices : (pair + 1) * slices] = scaled
    picked[...] = stats


def scale_kernel(floor, gathered, *refs):
    *picked, out, buf, sems = refs
    total = picked[0][...]
    for other in picked[1:]:
        total = total + other[...]
    factor = jnp.sqrt(jnp.maximum(total, floor))[:, out.shape[2] - 1 :]
    pieces = sems.shape[0]
    size = gathered.shape[0] // pieces
    copies = []
    for i in range(pieces):
        part = slice(i * size, (i + 1) * size)
        buf[part] = gathered[part] * factor[None]
        copies.append(pltpu.make_async_copy(buf.at[part], out.at[part], sems.at[i]))
        copies[-1].start()
    for copy in copies:
        copy.wait()


SMALL = pltpu.CompilerParams(vmem_limit_bytes=4 << 20)


def on_device(near_groups, far_groups, propagator, site_coords, momenta, source_slice):
    _, sinks, sources, _, slices, local_sites = propagator.shape
    pairs = sinks * sources
    lanes = 2 * momenta.shape[1]
    near = len(near_groups[0])
    far = len(far_groups[0])
    times = lax.axis_size("ta")
    rows = pairs * slices // near
    all_sites = float(local_sites * lax.axis_size(SITE_AXES))
    blocks = project(propagator, site_coords, momenta, source_slice, near)
    received = exchange(blocks.reshape(near, rows + 1, 1, lanes), SITE_AXES, near_groups)
    blocks = pl.pallas_call(
        functools.partial(near_kernel, near, far),
        out_shape=jax.ShapeDtypeStruct((far * (rows + 1), lanes), jnp.float32),
        in_specs=[IN_VMEM],
        out_specs=IN_VMEM,
        compiler_params=SMALL,
    )(received.reshape(near * (rows + 1), lanes))
    received = exchange(blocks.reshape(far, rows + 1, 1, lanes), "xy", far_groups)
    scaled, picked = pl.pallas_call(
        functools.partial(far_kernel, far, slices, all_sites),
        out_shape=(
            jax.ShapeDtypeStruct((near, rows, lanes), jnp.float32),
            jax.ShapeDtypeStruct((1, lanes), jnp.float32),
        ),
        in_specs=[IN_VMEM],
        out_specs=(IN_VMEM, IN_VMEM),
        compiler_params=SMALL,
    )(received.reshape(far * (rows + 1), lanes))
    gathered = exchange(scaled, SITE_AXES, near_groups)
    totals = [picked]
    for k in range(1, times):
        swap = [(t, t ^ k) for t in range(times)]
        totals.append(lax.ppermute(picked, "ta", swap))
    correlator = pl.pallas_call(
        functools.partial(scale_kernel, all_sites),
        out_shape=jax.ShapeDtypeStruct((pairs, slices, lanes), jnp.float32),
        in_specs=[IN_VMEM] * (1 + times),
        out_specs=pl.BlockSpec(memory_space=pltpu.HBM),
        scratch_shapes=[
            pltpu.VMEM((pairs, slices, lanes), jnp.float32),
            pltpu.SemaphoreType.DMA((4,)),
        ],
        compiler_params=SMALL,
    )(gathered.reshape(pairs, slices, lanes), *totals)
    return correlator


def solution(mesh):
    near_groups, far_groups = groups(mesh.shape["xy"], mesh.shape["gz"])
    return jax.shard_map(
        functools.partial(on_device, near_groups, far_groups),
        mesh=mesh,
        in_specs=(P(None, None, None, None, "ta", SITE_AXES), P(None, SITE_AXES), P(), P()),
        out_specs=P(None, "ta", None),
        check_vma=False,
    )
```

time: 74.6 us -> 64.9 us (0.87)
  blocking collectives: 16.6 us -> 39.6 us
  waiting for transfers between devices: 22.9 us -> 2.14 us
  starting transfers between devices: 24.4 us -> 16.7 us
  other arithmetic: 5.71 us -> 0 us
  Pallas kernels: 0 us -> 5.33 us
  local copies, waits for them, and re-layouts: 3.02 us -> 0 us
  matrix products: 0.79 us -> 0 us
  between operations: 0.82 us -> 0.05 us
    all_to_all x1 -> x2, blocking collectives: 16.6 us -> 39.6 us  [exchange(): lax.all_to_all(x, axes, split_axis=0, concat_axis=0, tiled=True, axis_ind...]
    all_to_all x3 -> x1, waiting for transfers between devices: 22.9 us -> 0.01 us  [exchange(): lax.all_to_all(x, axes, split_axis=0, concat_axis=0, tiled=True, axis_ind...]
    all_to_all x3 -> x1, starting transfers between devices: 24.4 us -> 7.74 us  [exchange(): lax.all_to_all(x, axes, split_axis=0, concat_axis=0, tiled=True, axis_ind...]
    ppermute x0 -> x3, starting transfers between devices: none -> 8.97 us  [on_device(): totals.append(lax.ppermute(picked, 'ta', swap))]
    pallas_call x0 -> x4, Pallas kernels: none -> 5.33 us  [the longest x1 3.66 us: project(): pl.pallas_call(functools.partial(project_kernel, near), out_shape=jax.Sha...]
    reduce_sum x6 -> x0, other arithmetic: 4.88 us -> none  [the longest x1 3.16 us: on_device(): jnp.sum(jnp.square(propagator), axis=(0, 3))]
    ppermute x0 -> x3, waiting for transfers between devices: none -> 2.13 us  [on_device(): totals.append(lax.ppermute(picked, 'ta', swap))]
    broadcast_in_dim x3 -> x0, local copies, waits for them, and re-layouts: 1.46 us -> none  [copies(): return jnp.broadcast_to(x, (lax.axis_size(axes), *x.shape))]
  transfers between devices with their start and end apart: 3 -> 4, of which waited for: 3 -> 2; matrix products, arithmetic and copies ran while one was open for 1% -> 0% of each run, Pallas kernels for 0% -> 0%
where the time goes in v2:
time: 64.9 us; the launch traced here: 63.9 us
  blocking collectives  39.6 us (61%)
  starting transfers between devices  16.7 us (26%)
  Pallas kernels  5.33 us (8%)
  waiting for transfers between devices  2.14 us (3%)
    all_to_all x2, blocking collectives, exchange(): lax.all_to_all(x, axes, split_axis=0, concat_axis=0, tiled=True, axis_ind...  39.6 us
    ppermute x3, starting transfers between devices, on_device(): totals.append(lax.ppermute(picked, 'ta', swap))  8.97 us
    all_to_all x1, starting transfers between devices, exchange(): lax.all_to_all(x, axes, split_axis=0, concat_axis=0, tiled=True, axis_ind...  7.74 us
    pallas_call x1, Pallas kernels, project(): pl.pallas_call(functools.partial(project_kernel, near), out_shape=jax.Sha...  3.66 us
    ppermute x3, waiting for transfers between devices, on_device(): totals.append(lax.ppermute(picked, 'ta', swap))  2.13 us
  transfers between devices with their start and end apart: 4, of which 2 were waited for; matrix products, arithmetic and copies ran while one was open for 0% of the time, Pallas kernels for 0%

profile of v2, /device:TPU:1, one launch (start us, length us, event | category | flops | bytes accessed | tf_op | source)
XLA Modules:
  0.0 63.9 jit_solution(3345030232014075117)
XLA Ops:
  0.0 3.7 %shard_map.46 = f32[528,128]{1,0:T(8,128)S(1)} custom-call(f32[2,4,4,9,32,128]{5,4,3,2,1,0:T(8,128)} %propagator.1, s32[3,128]{1,0:T(4,128)} %coords.1, s32[3,64]{1,0:T(4,128)} %momenta.1, s32[4]{0:T(128)} %source.1), custom_call_target="tpu_custom_call" | custom-call | tf_op jit(solution)/shard_map/pallas_call | solution.py:128
  3.7 16.6 %all_to_all.15 = f32[16,33,1,128]{3,2,1,0:T(1,128)S(1)} all-to-all(f32[16,33,1,128]{3,2,1,0:T(1,128)S(1)} %bitcast.4), channel_id=1, replica_groups={{0,1,2,3,4,5,6,7,8,9,10,11,12,13,14,15},{16,17,18,19,20,21,22,23,24,25,..., dimensions={0} | all-to-all | bytes 540672 | tf_op jit(solution)/shard_map/all_to_all | solution.py:32
  20.3 23.0 %all_to_all.16 = f32[8,33,1,128]{3,2,1,0:T(1,128)S(1)} all-to-all(f32[8,33,1,128]{3,2,1,0:T(1,128)S(1)} %bitcast.6), channel_id=1, replica_groups={{0,16,32,48,72,88,104,120},{8,24,40,56,64,80,96,112},{1,17,33,49,73,89,..., dimensions={0} | all-to-all | bytes 270336 | tf_op jit(solution)/shard_map/all_to_all | solution.py:32
  43.3 0.8 %shard_map.48 = (f32[16,32,128]{2,1,0:T(8,128)}, f32[1,128]{1,0:T(1,128)S(1)}) custom-call(f32[264,128]{1,0:T(8,128)S(1)} %bitcast.7), custom_call_target="tpu_custom_call" | custom-call | tf_op jit(solution)/shard_map/pallas_call | solution.py:218
  44.2 7.7 %all-to-all-start.2 = ((f32[16,32,128]{2,1,0:T(8,128)}), f32[16,32,128]{2,1,0:T(8,128)S(1)}, u32[]{:S(2)}, u32[]{:S(2)}) async-start(f32[16,32,128]{2,1,0:T(8,128)} %get-tuple-element.7), calls=%async_computation.2 | async-start | bytes 524288 | tf_op jit(solution)/shard_map/all_to_all | solution.py:32
  51.9 4.4 %collective-permute-start.2 = (f32[1,128]{1,0:T(1,128)S(1)}, f32[1,128]{1,0:T(1,128)S(1)}, u32[]{:S(2)}, u32[]{:S(2)}) collective-permute-start(f32[1,128]{1,0:T(1,128)S(1)} %get-tuple-element.8.refs_0_), channel_id=1, source_target_pairs={{0,384},{128,256},{256,128},{384,0},{1,385},{129,257},{257,129},{3... | collective-permute-start | bytes 1544 | tf_op jit(solution)/shard_map/ppermute | solution.py:232
  56.3 2.4 %collective-permute-start.1 = (f32[1,128]{1,0:T(1,128)S(1)}, f32[1,128]{1,0:T(1,128)S(1)}, u32[]{:S(2)}, u32[]{:S(2)}) collective-permute-start(f32[1,128]{1,0:T(1,128)S(1)} %get-tuple-element.8.refs_0_), channel_id=1, source_target_pairs={{0,256},{128,384},{256,0},{384,128},{1,257},{129,385},{257,1},{385... | collective-permute-start | bytes 1544 | tf_op jit(solution)/shard_map/ppermute | solution.py:232
  58.7 2.2 %collective-permute-start = (f32[1,128]{1,0:T(1,128)S(1)}, f32[1,128]{1,0:T(1,128)S(1)}, u32[]{:S(2)}, u32[]{:S(2)}) collective-permute-start(f32[1,128]{1,0:T(1,128)S(1)} %get-tuple-element.8.refs_0_), channel_id=1, source_target_pairs={{0,128},{128,0},{256,384},{384,256},{1,129},{129,1},{257,385},{385... | collective-permute-start | bytes 1544 | tf_op jit(solution)/shard_map/ppermute | solution.py:232
  60.9 0.0 collective-permute-done.2.refs_3_
  60.9 1.2 %collective-permute-done.1.refs_2_ = f32[1,128]{1,0:T(1,128)S(1)} collective-permute-done((f32[1,128]{1,0:T(1,128)S(1)}, f32[1,128]{1,0:T(1,128)S(1)}, u32[]{:S(2)}, u32[]{:S(2)}) %collective-permute-start.1) | collective-permute-done | bytes 544 | tf_op jit(solution)/shard_map/ppermute | solution.py:232
  62.1 0.9 %collective-permute-done.refs_1_ = f32[1,128]{1,0:T(1,128)S(1)} collective-permute-done((f32[1,128]{1,0:T(1,128)S(1)}, f32[1,128]{1,0:T(1,128)S(1)}, u32[]{:S(2)}, u32[]{:S(2)}) %collective-permute-start) | collective-permute-done | bytes 544 | tf_op jit(solution)/shard_map/ppermute | solution.py:232
  63.0 0.0 all-to-all-done.2.gathered
  63.0 0.8 %shard_map.49 = f32[16,32,128]{2,1,0:T(8,128)} custom-call(f32[16,32,128]{2,1,0:T(8,128)S(1)} %all-to-all-done.2.gathered, f32[1,128]{1,0:T(1,128)S(1)} %get-tuple-element.8.refs_0_, f32[1,128]{1,0:T(1,128)S(1)} %collective-permute-done.refs_1_, f32[1,128]{1,0:T(1,128)S(1)} %collective-permute-done.1.refs_2_, f32[1,128]{1,0:T(1,128)S(1)} %collective-permute-done.2.refs_3_), custom_call_target="tpu_custom_call" | custom-call | tf_op jit(solution)/shard_map/pallas_call | solution.py:233
  (1 shorter events, 0.0 us)
Async XLA Ops:
  44.2 18.9 %all-to-all-start.2 = ((f32[16,32,128]{2,1,0:T(8,128)}), f32[16,32,128]{2,1,0:T(8,128)S(1)}, u32[]{:S(2)}, u32[]{:S(2)}) async-start(f32[16,32,128]{2,1,0:T(8,128)} %get-tuple-element.7), calls=%async_computation.2 | async-start | bytes 524288 | tf_op jit(solution)/shard_map/all_to_all | solution.py:32
  51.9 9.0 %collective-permute-start.2 = (f32[1,128]{1,0:T(1,128)S(1)}, f32[1,128]{1,0:T(1,128)S(1)}, u32[]{:S(2)}, u32[]{:S(2)}) collective-permute-start(f32[1,128]{1,0:T(1,128)S(1)} %get-tuple-element.8.refs_0_), channel_id=1, source_target_pairs={{0,384},{128,256},{256,128},{384,0},{1,385},{129,257},{257,129},{3... | collective-permute-start | bytes 1544 | tf_op jit(solution)/shard_map/ppermute | solution.py:232
  56.3 5.8 %collective-permute-start.1 = (f32[1,128]{1,0:T(1,128)S(1)}, f32[1,128]{1,0:T(1,128)S(1)}, u32[]{:S(2)}, u32[]{:S(2)}) collective-permute-start(f32[1,128]{1,0:T(1,128)S(1)} %get-tuple-element.8.refs_0_), channel_id=1, source_target_pairs={{0,256},{128,384},{256,0},{384,128},{1,257},{129,385},{257,1},{385... | collective-permute-start | bytes 1544 | tf_op jit(solution)/shard_map/ppermute | solution.py:232
  58.7 4.3 %collective-permute-start = (f32[1,128]{1,0:T(1,128)S(1)}, f32[1,128]{1,0:T(1,128)S(1)}, u32[]{:S(2)}, u32[]{:S(2)}) collective-permute-start(f32[1,128]{1,0:T(1,128)S(1)} %get-tuple-element.8.refs_0_), channel_id=1, source_target_pairs={{0,128},{128,0},{256,384},{384,256},{1,129},{129,1},{257,385},{385... | collective-permute-start | bytes 1544 | tf_op jit(solution)/shard_map/ppermute | solution.py:232

commit v3 on v2

--- a/solution.py
+++ b/solution.py
@@ -14,17 +14,16 @@
 IN_VMEM = pl.BlockSpec(memory_space=pltpu.VMEM)
 
 
-def plane(pair, member, pairs):
-    return 2 * pair + (member if 2 * pair < pairs else 1 - member)
-
-
 def groups(planes, blocks):
     pairs = planes // 2
-    near = [
-        [plane(p, m, pairs) * blocks + g for m in range(2) for g in range(blocks)]
-        for p in range(pairs)
-    ]
-    far = [[plane(p, m, pairs) for p in range(pairs)] for m in range(2)]
+    swapped = range(pairs // 4, pairs - pairs // 4)
+    plane = [[2 * p + (m ^ (p in swapped)) for m in range(2)] for p in range(pairs)]
+    alternate = [b for start in (0, blocks // 2) for b in range(start, start + blocks // 2)]
+    alternate = [alternate[(i % 2) * (blocks // 2) + i // 2] for i in range(blocks)]
+    cores = [b for core in range(2) for b in alternate if b % 2 == core]
+    near = [[plane[p][m] * blocks + b for b in cores for m in range(2)] for p in range(pairs)]
+    half = pairs // 2
+    far = [[plane[(i % 2) * half + i // 2][m] for i in range(pairs)] for m in range(2)]
     return near, far
 
 
@@ -53,10 +52,11 @@
 
 def project_kernel(
     near, propagator, coords, momenta, source, out, parts, site_buf, mom_buf, src_buf, density,
-    total, part_sem, small_sem,
+    part_sem, small_sem,
 ):
     _, sinks, sources, colors, slices, _ = propagator.shape
     pairs = sinks * sources
+    step = pairs // part_sem.shape[0]
     lanes = out.shape[1]
     rows = pairs * slices // near
     loads = [
@@ -68,9 +68,11 @@
         load.start()
     copies = [
         pltpu.make_async_copy(
-            propagator.at[:, p // sources, p % sources], parts.at[p], part_sem.at[p]
+            propagator.at[:, p // sources, pl.ds(p % sources, step)],
+            parts.at[:, pl.ds(p, step)],
+            part_sem.at[p // step],
         )
-        for p in range(pairs)
+        for p in range(0, pairs, step)
     ]
     for copy in copies:
         copy.start()
@@ -78,70 +80,58 @@
         load.wait()
     phases = phase_table(site_buf[...].astype(jnp.float32), mom_buf[...].astype(jnp.float32))
     first = lax.axis_index("ta") * slices
-    lane = lax.broadcasted_iota(jnp.int32, (8, lanes), 1)
-    counts = jnp.zeros((8, lanes), jnp.float32)
+    row = lax.broadcasted_iota(jnp.int32, (slices, lanes), 0)
+    lane = lax.broadcasted_iota(jnp.int32, (slices, lanes), 1)
+    weight = jnp.zeros((slices, lanes), jnp.float32)
     for i in range(source.shape[0]):
-        counts = counts + jnp.where(lane == src_buf[i] - first, 1.0, 0.0)
-    total[...] = jnp.zeros_like(total)
-    step = 4
+        weight = weight + jnp.where(row == src_buf[i] - first, 1.0, 0.0)
+    weight = jnp.where(lane < slices, jnp.where(row == lane, 1.0, 0.0), weight)
     over_pairs = None
     for p in range(pairs):
-        copies[p].wait()
+        if p % step == 0:
+            copies[p // step].wait()
         value = None
         for r in range(2):
             for c in range(colors):
-                part = parts[p, r, c]
+                part = parts[r, p, c]
                 value = part * part if value is None else value + part * part
         density[p * slices : (p + 1) * slices] = value
         over_pairs = value if over_pairs is None else over_pairs + value
-        if p % step == step - 1:
-            begin = (p + 1 - step) * slices
-            projected = jnp.dot(
-                density[begin : begin + step * slices],
-                phases,
-                precision=lax.Precision.HIGHEST,
-                preferred_element_type=jnp.float32,
-            )
-            for part in range(step * slices // rows):
-                block = begin // rows + part
-                out[block * (rows + 1) : block * (rows + 1) + rows] = projected[
-                    part * rows : (part + 1) * rows
-                ]
-    total[:slices] = over_pairs
-    by_slice = lax.dot_general(
-        jnp.ones((8, total.shape[1]), jnp.float32),
-        total[...],
-        (((1,), (1,)), ((), ())),
+    by_slice = jnp.sum(over_pairs, axis=1, keepdims=True)
+    stats = jnp.sum(by_slice * weight, axis=0, keepdims=True)
+    projected = jnp.dot(
+        density[...],
+        phases,
         precision=lax.Precision.HIGHEST,
         preferred_element_type=jnp.float32,
     )
-    picked = jnp.sum(by_slice * counts, axis=1, keepdims=True)
-    stats = jnp.where(lane < slices, by_slice, picked)
     for block in range(near):
-        out[block * (rows + 1) + rows : (block + 1) * (rows + 1)] = stats[:1]
+        begin = block * (rows + 1)
+        out[begin : begin + rows] = projected[block * rows : (block + 1) * rows]
+        out[begin + rows : begin + rows + 1] = stats
 
 
 def project(propagator, coords, momenta, source, near):
     _, sinks, sources, colors, slices, sites = propagator.shape
     pairs = sinks * sources
     lanes = 2 * momenta.shape[1]
+    arrays = (propagator, coords, momenta, source)
     return pl.pallas_call(
         functools.partial(project_kernel, near),
         out_shape=jax.ShapeDtypeStruct((pairs * slices + near, lanes), jnp.float32),
         in_specs=[IN_HBM] * 4,
         out_specs=IN_VMEM,
         scratch_shapes=[
-            pltpu.VMEM((pairs, 2, colors, slices, sites), jnp.float32),
+            pltpu.VMEM((2, pairs, colors, slices, sites), jnp.float32),
             pltpu.VMEM(coords.shape, jnp.int32),
             pltpu.VMEM(momenta.shape, jnp.int32),
             pltpu.SMEM(source.shape, jnp.int32),
             pltpu.VMEM((pairs * slices, sites), jnp.float32),
-            pltpu.VMEM((lanes, sites), jnp.float32),
-            pltpu.SemaphoreType.DMA((pairs,)),
+            pltpu.SemaphoreType.DMA((pairs // 2,)),
             pltpu.SemaphoreType.DMA((3,)),
         ],
         compiler_params=pltpu.CompilerParams(vmem_limit_bytes=12 << 20),
-    )(*[pltpu.with_memory_space_constraint(x, pltpu.HBM) for x in (propagator, coords, momenta, source)])
+    )(*[pltpu.with_memory_space_constraint(x, pltpu.HBM) for x in arrays])
 
 
 def sum_of_blocks(ref, blocks):
@@ -175,12 +165,8 @@
     picked[...] = stats
 
 
-def scale_kernel(floor, gathered, *refs):
-    *picked, out, buf, sems = refs
-    total = picked[0][...]
-    for other in picked[1:]:
-        total = total + other[...]
-    factor = jnp.sqrt(jnp.maximum(total, floor))[:, out.shape[2] - 1 :]
+def scale_kernel(floor, gathered, total, out, buf, sems):
+    factor = jnp.sqrt(jnp.maximum(total[...], floor))[:, out.shape[2] - 1 :]
     pieces = sems.shape[0]
     size = gathered.shape[0] // pieces
     copies = []
@@ -202,7 +188,6 @@
     lanes = 2 * momenta.shape[1]
     near = len(near_groups[0])
     far = len(far_groups[0])
-    times = lax.axis_size("ta")
     rows = pairs * slices // near
     all_sites = float(local_sites * lax.axis_size(SITE_AXES))
     blocks = project(propagator, site_coords, momenta, source_slice, near)
@@ -226,21 +211,18 @@
         compiler_params=SMALL,
     )(received.reshape(far * (rows + 1), lanes))
     gathered = exchange(scaled, SITE_AXES, near_groups)
-    totals = [picked]
-    for k in range(1, times):
-        swap = [(t, t ^ k) for t in range(times)]
-        totals.append(lax.ppermute(picked, "ta", swap))
+    picked = lax.psum(picked, "ta")
     correlator = pl.pallas_call(
         functools.partial(scale_kernel, all_sites),
         out_shape=jax.ShapeDtypeStruct((pairs, slices, lanes), jnp.float32),
-        in_specs=[IN_VMEM] * (1 + times),
+        in_specs=[IN_VMEM] * 2,
         out_specs=pl.BlockSpec(memory_space=pltpu.HBM),
         scratch_shapes=[
             pltpu.VMEM((pairs, slices, lanes), jnp.float32),
-            pltpu.SemaphoreType.DMA((4,)),
+            pltpu.SemaphoreType.DMA((2,)),
         ],
         compiler_params=SMALL,
-    )(gathered.reshape(pairs, slices, lanes), *totals)
+    )(gathered.reshape(pairs, slices, lanes), picked)
     return correlator
 
 

time: 64.9 us -> 60 us (0.924)
  starting transfers between devices: 16.7 us -> 7.82 us
  blocking collectives: 39.6 us -> 46.7 us
  waiting for transfers between devices: 2.14 us -> 0.01 us
  Pallas kernels: 5.33 us -> 4.49 us
    ppermute x3 -> x0, starting transfers between devices: 8.97 us -> none  [on_device(): totals.append(lax.ppermute(picked, 'ta', swap))]
    psum x0 -> x1, blocking collectives: none -> 8.75 us  [on_device(): picked = lax.psum(picked, 'ta')]
    ppermute x3 -> x0, waiting for transfers between devices: 2.13 us -> none  [on_device(): totals.append(lax.ppermute(picked, 'ta', swap))]
    all_to_all x2, blocking collectives: 39.6 us -> 37.9 us  [exchange(): lax.all_to_all(x, axes, split_axis=0, concat_axis=0, tiled=True, axis_ind...]
    pallas_call x1, Pallas kernels: 3.66 us -> 2.84 us  [project(): pl.pallas_call(functools.partial(project_kernel, near), out_shape=jax.Sha...]
  transfers between devices with their start and end apart: 4 -> 1, of which waited for: 2 -> 0; matrix products, arithmetic and copies ran while one was open for 0% -> 0% of each run, Pallas kernels for 0% -> 0%
where the time goes in v3:
time: 60 us; the launch traced here: 59 us
  blocking collectives  46.7 us (78%)
  starting transfers between devices  7.82 us (13%)
  Pallas kernels  4.49 us (7%)
    all_to_all x2, blocking collectives, exchange(): lax.all_to_all(x, axes, split_axis=0, concat_axis=0, tiled=True, axis_ind...  37.9 us
    psum x1, blocking collectives, on_device(): picked = lax.psum(picked, 'ta')  8.75 us
    all_to_all x1, starting transfers between devices, exchange(): lax.all_to_all(x, axes, split_axis=0, concat_axis=0, tiled=True, axis_ind...  7.82 us
    pallas_call x1, Pallas kernels, project(): pl.pallas_call(functools.partial(project_kernel, near), out_shape=jax.Sha...  2.84 us
  transfers between devices with their start and end apart: 1, of which 0 were waited for; matrix products, arithmetic and copies ran while one was open for 0% of the time, Pallas kernels for 0%

profile of v3, /device:TPU:1, one launch (start us, length us, event | category | flops | bytes accessed | tf_op | source)
XLA Modules:
  0.0 59.0 jit_solution(14468278691797464297)
XLA Ops:
  0.0 2.8 %shard_map.46 = f32[528,128]{1,0:T(8,128)S(1)} custom-call(f32[2,4,4,9,32,128]{5,4,3,2,1,0:T(8,128)} %propagator.1, s32[3,128]{1,0:T(4,128)} %coords.1, s32[3,64]{1,0:T(4,128)} %momenta.1, s32[4]{0:T(128)} %source.1), custom_call_target="tpu_custom_call" | custom-call | tf_op jit(solution)/shard_map/pallas_call | solution.py:119
  2.8 16.2 %all_to_all.15 = f32[16,33,1,128]{3,2,1,0:T(1,128)S(1)} all-to-all(f32[16,33,1,128]{3,2,1,0:T(1,128)S(1)} %bitcast.4), channel_id=1, replica_groups={{0,8,4,12,2,10,6,14,1,9,5,13,3,11,7,15},{16,24,20,28,18,26,22,30,17,25,..., dimensions={0} | all-to-all | bytes 540672 | tf_op jit(solution)/shard_map/all_to_all | solution.py:31
  19.1 21.7 %all_to_all.16 = f32[8,33,1,128]{3,2,1,0:T(1,128)S(1)} all-to-all(f32[8,33,1,128]{3,2,1,0:T(1,128)S(1)} %bitcast.6), channel_id=1, replica_groups={{0,72,16,88,40,96,56,112},{8,64,24,80,32,104,48,120},{1,73,17,89,41,97,..., dimensions={0} | all-to-all | bytes 270336 | tf_op jit(solution)/shard_map/all_to_all | solution.py:31
  40.8 0.8 %shard_map.48 = (f32[16,32,128]{2,1,0:T(8,128)}, f32[1,128]{1,0:T(1,128)S(1)}) custom-call(f32[264,128]{1,0:T(8,128)S(1)} %bitcast.7), custom_call_target="tpu_custom_call" | custom-call | tf_op jit(solution)/shard_map/pallas_call | solution.py:203
  41.6 7.8 %all-to-all-start.2 = ((f32[16,32,128]{2,1,0:T(8,128)}), f32[16,32,128]{2,1,0:T(8,128)S(1)}, u32[]{:S(2)}, u32[]{:S(2)}) async-start(f32[16,32,128]{2,1,0:T(8,128)} %get-tuple-element.7), calls=%async_computation.2 | async-start | bytes 524288 | tf_op jit(solution)/shard_map/all_to_all | solution.py:31
  49.5 8.8 %psum.7.total = f32[1,128]{1,0:T(1,128)S(1)} all-reduce(f32[1,128]{1,0:T(1,128)S(1)} %get-tuple-element.8), channel_id=1, replica_groups=mesh['ta'=4,'xy'=16,'gz'=8] {'ta'}, use_global_device_ids=true, to_apply=%region_0.0 | all-reduce | flops 128 | bytes 1024 | tf_op jit(solution)/shard_map/psum | solution.py:214
  58.2 0.0 all-to-all-done.2.gathered
  58.2 0.8 %shard_map.49 = f32[16,32,128]{2,1,0:T(8,128)} custom-call(f32[16,32,128]{2,1,0:T(8,128)S(1)} %all-to-all-done.2.gathered, f32[1,128]{1,0:T(1,128)S(1)} %psum.7.total), custom_call_target="tpu_custom_call" | custom-call | tf_op jit(solution)/shard_map/pallas_call | solution.py:215
  (1 shorter events, 0.0 us)
Async XLA Ops:
  41.6 16.6 %all-to-all-start.2 = ((f32[16,32,128]{2,1,0:T(8,128)}), f32[16,32,128]{2,1,0:T(8,128)S(1)}, u32[]{:S(2)}, u32[]{:S(2)}) async-start(f32[16,32,128]{2,1,0:T(8,128)} %get-tuple-element.7), calls=%async_computation.2 | async-start | bytes 524288 | tf_op jit(solution)/shard_map/all_to_all | solution.py:31

commit v4 on v3

--- a/solution.py
+++ b/solution.py
@@ -51,8 +51,8 @@
 
 
 def project_kernel(
-    near, propagator, coords, momenta, source, out, parts, site_buf, mom_buf, src_buf, density,
-    part_sem, small_sem,
+    near, propagator, coords, momenta, source, out, mine, parts, site_buf, mom_buf, src_buf,
+    density, blocks, part_sem, small_sem, out_sem,
 ):
     _, sinks, sources, colors, slices, _ = propagator.shape
     pairs = sinks * sources
@@ -99,16 +99,27 @@
         over_pairs = value if over_pairs is None else over_pairs + value
     by_slice = jnp.sum(over_pairs, axis=1, keepdims=True)
     stats = jnp.sum(by_slice * weight, axis=0, keepdims=True)
+    mine[...] = stats
     projected = jnp.dot(
         density[...],
         phases,
         precision=lax.Precision.HIGHEST,
         preferred_element_type=jnp.float32,
     )
+    stores = []
+    size = blocks.shape[0] // out_sem.shape[0]
     for block in range(near):
         begin = block * (rows + 1)
-        out[begin : begin + rows] = projected[block * rows : (block + 1) * rows]
-        out[begin + rows : begin + rows + 1] = stats
+        blocks[begin : begin + rows] = projected[block * rows : (block + 1) * rows]
+        blocks[begin + rows : begin + rows + 1] = stats
+        if (begin + rows + 1) % size == 0:
+            part = pl.ds(size * len(stores), size)
+            stores.append(
+                pltpu.make_async_copy(blocks.at[part], out.at[part], out_sem.at[len(stores)])
+            )
+            stores[-1].start()
+    for store in stores:
+        store.wait()
 
 
 def project(propagator, coords, momenta, source, near):
@@ -118,17 +129,22 @@
     arrays = (propagator, coords, momenta, source)
     return pl.pallas_call(
         functools.partial(project_kernel, near),
-        out_shape=jax.ShapeDtypeStruct((pairs * slices + near, lanes), jnp.float32),
+        out_shape=(
+            jax.ShapeDtypeStruct((pairs * slices + near, lanes), jnp.float32),
+            jax.ShapeDtypeStruct((1, lanes), jnp.float32),
+        ),
         in_specs=[IN_HBM] * 4,
-        out_specs=IN_VMEM,
+        out_specs=(IN_HBM, IN_VMEM),
         scratch_shapes=[
             pltpu.VMEM((2, pairs, colors, slices, sites), jnp.float32),
             pltpu.VMEM(coords.shape, jnp.int32),
             pltpu.VMEM(momenta.shape, jnp.int32),
             pltpu.SMEM(source.shape, jnp.int32),
             pltpu.VMEM((pairs * slices, sites), jnp.float32),
+            pltpu.VMEM((pairs * slices + near, lanes), jnp.float32),
             pltpu.SemaphoreType.DMA((pairs // 2,)),
             pltpu.SemaphoreType.DMA((3,)),
+            pltpu.SemaphoreType.DMA((2,)),
         ],
         compiler_params=pltpu.CompilerParams(vmem_limit_bytes=12 << 20),
     )(*[pltpu.with_memory_space_constraint(x, pltpu.HBM) for x in arrays])
@@ -142,14 +158,17 @@
     return value
 
 
-def near_kernel(near, far, received, out):
+def near_kernel(near, far, slices, received, picked, out):
     value = sum_of_blocks(received, near)
-    rows = value.shape[0]
+    rows, lanes = value.shape
+    lane = lax.broadcasted_iota(jnp.int32, (1, lanes), 1)
+    stats = jnp.where(lane < slices, value[rows - 1 :], picked[...])
     for b in range(far):
-        out[b * rows : (b + 1) * rows] = value
-
-
-def far_kernel(far, slices, floor, received, out, picked):
+        out[b * rows : (b + 1) * rows - 1] = value[: rows - 1]
+        out[(b + 1) * rows - 1 : (b + 1) * rows] = stats
+
+
+def far_kernel(near, far, slices, floor, received, out):
     value = sum_of_blocks(received, far)
     rows = value.shape[0] - 1
     lanes = value.shape[1]
@@ -160,19 +179,27 @@
     norm = jnp.maximum(column, floor)
     for pair in range(rows // slices):
         scaled = value[pair * slices : (pair + 1) * slices] / norm
-        for b in range(out.shape[0]):
-            out[b, pair * slices : (pair + 1) * slices] = scaled
-    picked[...] = stats
-
-
-def scale_kernel(floor, gathered, total, out, buf, sems):
-    factor = jnp.sqrt(jnp.maximum(total[...], floor))[:, out.shape[2] - 1 :]
+        for b in range(near):
+            begin = b * (rows + 1) + pair * slices
+            out[begin : begin + slices] = scaled
+    for b in range(near):
+        out[b * (rows + 1) + rows : (b + 1) * (rows + 1)] = stats
+
+
+def scale_kernel(near, floor, gathered, out, buf, sems):
+    rows = gathered.shape[0] // near - 1
+    total = gathered[rows : rows + 1]
+    for b in range(1, near):
+        total = total + gathered[b * (rows + 1) + rows : (b + 1) * (rows + 1)]
+    factor = jnp.sqrt(jnp.maximum(total, floor))[:, total.shape[1] - 1 :]
     pieces = sems.shape[0]
-    size = gathered.shape[0] // pieces
+    size = near // pieces
     copies = []
     for i in range(pieces):
-        part = slice(i * size, (i + 1) * size)
-        buf[part] = gathered[part] * factor[None]
+        for b in range(i * size, (i + 1) * size):
+            begin = b * (rows + 1)
+            buf[b * rows : (b + 1) * rows] = gathered[begin : begin + rows] * factor
+        part = pl.ds(i * size * rows, size * rows)
         copies.append(pltpu.make_async_copy(buf.at[part], out.at[part], sems.at[i]))
         copies[-1].start()
     for copy in copies:
@@ -190,40 +217,37 @@
     far = len(far_groups[0])
     rows = pairs * slices // near
     all_sites = float(local_sites * lax.axis_size(SITE_AXES))
-    blocks = project(propagator, site_coords, momenta, source_slice, near)
+    blocks, picked = project(propagator, site_coords, momenta, source_slice, near)
     received = exchange(blocks.reshape(near, rows + 1, 1, lanes), SITE_AXES, near_groups)
+    picked = lax.psum(picked, "ta")
     blocks = pl.pallas_call(
-        functools.partial(near_kernel, near, far),
+        functools.partial(near_kernel, near, far, slices),
         out_shape=jax.ShapeDtypeStruct((far * (rows + 1), lanes), jnp.float32),
+        in_specs=[IN_VMEM] * 2,
+        out_specs=IN_VMEM,
+        compiler_params=SMALL,
+    )(received.reshape(near * (rows + 1), lanes), picked)
+    received = exchange(blocks.reshape(far, rows + 1, 1, lanes), "xy", far_groups)
+    blocks = pl.pallas_call(
+        functools.partial(far_kernel, near, far, slices, all_sites),
+        out_shape=jax.ShapeDtypeStruct((near * (rows + 1), lanes), jnp.float32),
         in_specs=[IN_VMEM],
         out_specs=IN_VMEM,
         compiler_params=SMALL,
-    )(received.reshape(near * (rows + 1), lanes))
-    received = exchange(blocks.reshape(far, rows + 1, 1, lanes), "xy", far_groups)
-    scaled, picked = pl.pallas_call(
-        functools.partial(far_kernel, far, slices, all_sites),
-        out_shape=(
-            jax.ShapeDtypeStruct((near, rows, lanes), jnp.float32),
-            jax.ShapeDtypeStruct((1, lanes), jnp.float32),
-        ),
+    )(received.reshape(far * (rows + 1), lanes))
+    received = exchange(blocks.reshape(near, rows + 1, 1, lanes), SITE_AXES, near_groups)
+    correlator = pl.pallas_call(
+        functools.partial(scale_kernel, near, all_sites),
+        out_shape=jax.ShapeDtypeStruct((near * rows, lanes), jnp.float32),
         in_specs=[IN_VMEM],
-        out_specs=(IN_VMEM, IN_VMEM),
-        compiler_params=SMALL,
-    )(received.reshape(far * (rows + 1), lanes))
-    gathered = exchange(scaled, SITE_AXES, near_groups)
-    picked = lax.psum(picked, "ta")
-    correlator = pl.pallas_call(
-        functools.partial(scale_kernel, all_sites),
-        out_shape=jax.ShapeDtypeStruct((pairs, slices, lanes), jnp.float32),
-        in_specs=[IN_VMEM] * 2,
-        out_specs=pl.BlockSpec(memory_space=pltpu.HBM),
+        out_specs=IN_HBM,
         scratch_shapes=[
-            pltpu.VMEM((pairs, slices, lanes), jnp.float32),
+            pltpu.VMEM((near * rows, lanes), jnp.float32),
             pltpu.SemaphoreType.DMA((2,)),
         ],
         compiler_params=SMALL,
-    )(gathered.reshape(pairs, slices, lanes), picked)
-    return correlator
+    )(received.reshape(near * (rows + 1), lanes))
+    return correlator.reshape(pairs, slices, lanes)
 
 
 def solution(mesh):

time: 60 us -> 62.2 us (1.037); the launches traced: 59 us -> 61.9 us
  starting transfers between devices: 7.82 us -> 10.2 us
  waiting for transfers between devices: 0.01 us -> 0.65 us
    psum x1, blocking collectives: 8.75 us -> 6.29 us  [on_device(): picked = lax.psum(picked, 'ta')]
    all_to_all x1, starting transfers between devices: 7.82 us -> 10.2 us  [exchange(): lax.all_to_all(x, axes, split_axis=0, concat_axis=0, tiled=True, axis_ind...]
    all_to_all x2, blocking collectives: 37.9 us -> 40.2 us  [exchange(): lax.all_to_all(x, axes, split_axis=0, concat_axis=0, tiled=True, axis_ind...]
    all_to_all x1, waiting for transfers between devices: 0.01 us -> 0.65 us  [exchange(): lax.all_to_all(x, axes, split_axis=0, concat_axis=0, tiled=True, axis_ind...]
  transfers between devices with their start and end apart: 1 -> 1, of which waited for: 0 -> 1; matrix products, arithmetic and copies ran while one was open for 0% -> 0% of each run, Pallas kernels for 0% -> 0%
where the time goes in v4:
time: 62.2 us; the launch traced here: 61.9 us
  blocking collectives  46.5 us (75%)
  starting transfers between devices  10.2 us (16%)
  Pallas kernels  4.52 us (7%)
  waiting for transfers between devices  0.65 us (1%)
    all_to_all x2, blocking collectives, exchange(): lax.all_to_all(x, axes, split_axis=0, concat_axis=0, tiled=True, axis_ind...  40.2 us
    all_to_all x1, starting transfers between devices, exchange(): lax.all_to_all(x, axes, split_axis=0, concat_axis=0, tiled=True, axis_ind...  10.2 us
    psum x1, blocking collectives, on_device(): picked = lax.psum(picked, 'ta')  6.29 us
    pallas_call x1, Pallas kernels, project(): pl.pallas_call(functools.partial(project_kernel, near), out_shape=(jax.Sh...  3.53 us
  transfers between devices with their start and end apart: 1, of which 1 were waited for; matrix products, arithmetic and copies ran while one was open for 0% of the time, Pallas kernels for 0%

profile of v4, /device:TPU:1, one launch (start us, length us, event | category | flops | bytes accessed | tf_op | source)
XLA Modules:
  0.0 61.9 jit_solution(9219973094422047673)
XLA Ops:
  0.0 3.5 %shard_map.46 = (f32[528,128]{1,0:T(8,128)}, f32[1,128]{1,0:T(1,128)S(1)}) custom-call(f32[2,4,4,9,32,128]{5,4,3,2,1,0:T(8,128)} %propagator.1, s32[3,128]{1,0:T(4,128)} %coords.1, s32[3,64]{1,0:T(4,128)} %momenta.1, s32[4]{0:T(128)} %source.1), custom_call_target="tpu_custom_call" | custom-call | tf_op jit(solution)/shard_map/pallas_call | solution.py:130
  3.5 10.2 %all-to-all-start = ((f32[16,33,1,128]{3,2,1,0:T(1,128)}), f32[16,33,1,128]{3,2,1,0:T(1,128)S(1)}, u32[]{:S(2)}, u32[]{:S(2)}) async-start(f32[16,33,1,128]{3,2,1,0:T(1,128)} %bitcast), calls=%async_computation | async-start | bytes 540672 | tf_op jit(solution)/shard_map/all_to_all | solution.py:31
  13.8 6.3 %psum.7.picked = f32[1,128]{1,0:T(1,128)S(1)} all-reduce(f32[1,128]{1,0:T(1,128)S(1)} %get-tuple-element.8), channel_id=1, replica_groups=mesh['ta'=4,'xy'=16,'gz'=8] {'ta'}, use_global_device_ids=true, to_apply=%region_0.0 | all-reduce | flops 128 | bytes 1024 | tf_op jit(solution)/shard_map/psum | solution.py:222
  20.0 0.7 %all-to-all-done = f32[16,33,1,128]{3,2,1,0:T(1,128)S(1)} async-done(((f32[16,33,1,128]{3,2,1,0:T(1,128)}), f32[16,33,1,128]{3,2,1,0:T(1,128)S(1)}, u32[]{:S(2)}, u32[]{:S(2)}) %all-to-all-start) | async-done | bytes 270368 | tf_op jit(solution)/shard_map/all_to_all | solution.py:31
  20.7 22.9 %all_to_all.15 = f32[8,33,1,128]{3,2,1,0:T(1,128)S(1)} all-to-all(f32[8,33,1,128]{3,2,1,0:T(1,128)S(1)} %bitcast.10), channel_id=1, replica_groups={{0,72,16,88,40,96,56,112},{8,64,24,80,32,104,48,120},{1,73,17,89,41,97,..., dimensions={0} | all-to-all | bytes 270336 | tf_op jit(solution)/shard_map/all_to_all | solution.py:31
  43.6 0.1 shard_map.48
  43.8 17.3 %all_to_all.16 = f32[16,33,1,128]{3,2,1,0:T(1,128)S(1)} all-to-all(f32[16,33,1,128]{3,2,1,0:T(1,128)S(1)} %bitcast.8), channel_id=1, replica_groups={{0,8,4,12,2,10,6,14,1,9,5,13,3,11,7,15},{16,24,20,28,18,26,22,30,17,25,..., dimensions={0} | all-to-all | bytes 540672 | tf_op jit(solution)/shard_map/all_to_all | solution.py:31
  61.0 0.8 %shard_map.49 = f32[512,128]{1,0:T(8,128)} custom-call(f32[528,128]{1,0:T(8,128)S(1)} %bitcast.9), custom_call_target="tpu_custom_call" | custom-call | tf_op jit(solution)/shard_map/pallas_call | solution.py:239
  (1 shorter events, 0.0 us)
Async XLA Ops:
  3.5 17.2 %all-to-all-start = ((f32[16,33,1,128]{3,2,1,0:T(1,128)}), f32[16,33,1,128]{3,2,1,0:T(1,128)S(1)}, u32[]{:S(2)}, u32[]{:S(2)}) async-start(f32[16,33,1,128]{3,2,1,0:T(1,128)} %bitcast), calls=%async_computation | async-start | bytes 540672 | tf_op jit(solution)/shard_map/all_to_all | solution.py:31

commit v5 on v3

--- a/solution.py
+++ b/solution.py
@@ -16,14 +16,17 @@
 
 def groups(planes, blocks):
     pairs = planes // 2
-    swapped = range(pairs // 4, pairs - pairs // 4)
-    plane = [[2 * p + (m ^ (p in swapped)) for m in range(2)] for p in range(pairs)]
+    half = pairs // 2
+    plane = []
+    for p in range(pairs):
+        swapped = (p % half == half // 4) != (p >= half)
+        plane.append([2 * p + (m ^ swapped) for m in range(2)])
     alternate = [b for start in (0, blocks // 2) for b in range(start, start + blocks // 2)]
     alternate = [alternate[(i % 2) * (blocks // 2) + i // 2] for i in range(blocks)]
     cores = [b for core in range(2) for b in alternate if b % 2 == core]
     near = [[plane[p][m] * blocks + b for b in cores for m in range(2)] for p in range(pairs)]
-    half = pairs // 2
-    far = [[plane[(i % 2) * half + i // 2][m] for i in range(pairs)] for m in range(2)]
+    order = [*range(half, pairs), *reversed(range(half))]
+    far = [[plane[p][m] for p in order] for m in range(2)]
     return near, far
 
 

time: 60 us -> 55.6 us (0.927)
  blocking collectives: 46.7 us -> 44.4 us
  starting transfers between devices: 7.82 us -> 5.68 us
    all_to_all x2, blocking collectives: 37.9 us -> 35.7 us  [exchange(): lax.all_to_all(x, axes, split_axis=0, concat_axis=0, tiled=True, axis_ind...]
    all_to_all x1, starting transfers between devices: 7.82 us -> 5.68 us  [exchange(): lax.all_to_all(x, axes, split_axis=0, concat_axis=0, tiled=True, axis_ind...]
where the time goes in v5:
time: 55.6 us; the launch traced here: 54.6 us
  blocking collectives  44.4 us (80%)
  starting transfers between devices  5.68 us (10%)
  Pallas kernels  4.49 us (8%)
    all_to_all x2, blocking collectives, exchange(): lax.all_to_all(x, axes, split_axis=0, concat_axis=0, tiled=True, axis_ind...  35.7 us
    psum x1, blocking collectives, on_device(): picked = lax.psum(picked, 'ta')  8.75 us
    all_to_all x1, starting transfers between devices, exchange(): lax.all_to_all(x, axes, split_axis=0, concat_axis=0, tiled=True, axis_ind...  5.68 us
    pallas_call x1, Pallas kernels, project(): pl.pallas_call(functools.partial(project_kernel, near), out_shape=jax.Sha...  2.84 us
  transfers between devices with their start and end apart: 1, of which 0 were waited for; matrix products, arithmetic and copies ran while one was open for 0% of the time, Pallas kernels for 0%

profile of v5, /device:TPU:1, one launch (start us, length us, event | category | flops | bytes accessed | tf_op | source)
XLA Modules:
  0.0 54.6 jit_solution(7776448660553133377)
XLA Ops:
  0.0 2.8 %shard_map.46 = f32[528,128]{1,0:T(8,128)S(1)} custom-call(f32[2,4,4,9,32,128]{5,4,3,2,1,0:T(8,128)} %propagator.1, s32[3,128]{1,0:T(4,128)} %coords.1, s32[3,64]{1,0:T(4,128)} %momenta.1, s32[4]{0:T(128)} %source.1), custom_call_target="tpu_custom_call" | custom-call | tf_op jit(solution)/shard_map/pallas_call | solution.py:122
  2.8 16.2 %all_to_all.15 = f32[16,33,1,128]{3,2,1,0:T(1,128)S(1)} all-to-all(f32[16,33,1,128]{3,2,1,0:T(1,128)S(1)} %bitcast.4), channel_id=1, replica_groups={{0,8,4,12,2,10,6,14,1,9,5,13,3,11,7,15},{24,16,28,20,26,18,30,22,25,17,..., dimensions={0} | all-to-all | bytes 540672 | tf_op jit(solution)/shard_map/all_to_all | solution.py:34
  19.1 19.4 %all_to_all.16 = f32[8,33,1,128]{3,2,1,0:T(1,128)S(1)} all-to-all(f32[8,33,1,128]{3,2,1,0:T(1,128)S(1)} %bitcast.6), channel_id=1, replica_groups={{72,80,104,120,48,32,24,0},{64,88,96,112,56,40,16,8},{73,81,105,121,49,..., dimensions={0} | all-to-all | bytes 270336 | tf_op jit(solution)/shard_map/all_to_all | solution.py:34
  38.6 0.8 %shard_map.48 = (f32[16,32,128]{2,1,0:T(8,128)}, f32[1,128]{1,0:T(1,128)S(1)}) custom-call(f32[264,128]{1,0:T(8,128)S(1)} %bitcast.7), custom_call_target="tpu_custom_call" | custom-call | tf_op jit(solution)/shard_map/pallas_call | solution.py:206
  39.4 5.7 %all-to-all-start.2 = ((f32[16,32,128]{2,1,0:T(8,128)}), f32[16,32,128]{2,1,0:T(8,128)S(1)}, u32[]{:S(2)}, u32[]{:S(2)}) async-start(f32[16,32,128]{2,1,0:T(8,128)} %get-tuple-element.7), calls=%async_computation.2 | async-start | bytes 524288 | tf_op jit(solution)/shard_map/all_to_all | solution.py:34
  45.1 8.8 %psum.7.total = f32[1,128]{1,0:T(1,128)S(1)} all-reduce(f32[1,128]{1,0:T(1,128)S(1)} %get-tuple-element.8), channel_id=1, replica_groups=mesh['ta'=4,'xy'=16,'gz'=8] {'ta'}, use_global_device_ids=true, to_apply=%region_0.0 | all-reduce | flops 128 | bytes 1024 | tf_op jit(solution)/shard_map/psum | solution.py:217
  53.8 0.0 all-to-all-done.2.gathered
  53.8 0.8 %shard_map.49 = f32[16,32,128]{2,1,0:T(8,128)} custom-call(f32[16,32,128]{2,1,0:T(8,128)S(1)} %all-to-all-done.2.gathered, f32[1,128]{1,0:T(1,128)S(1)} %psum.7.total), custom_call_target="tpu_custom_call" | custom-call | tf_op jit(solution)/shard_map/pallas_call | solution.py:218
  (1 shorter events, 0.0 us)
Async XLA Ops:
  39.4 14.4 %all-to-all-start.2 = ((f32[16,32,128]{2,1,0:T(8,128)}), f32[16,32,128]{2,1,0:T(8,128)S(1)}, u32[]{:S(2)}, u32[]{:S(2)}) async-start(f32[16,32,128]{2,1,0:T(8,128)} %get-tuple-element.7), calls=%async_computation.2 | async-start | bytes 524288 | tf_op jit(solution)/shard_map/all_to_all | solution.py:34

commit v6 on v5

--- a/solution.py
+++ b/solution.py
@@ -12,6 +12,10 @@
 SITE_AXES = ("xy", "gz")
 IN_HBM = pl.BlockSpec(memory_space=pltpu.HBM)
 IN_VMEM = pl.BlockSpec(memory_space=pltpu.VMEM)
+
+
+NEAR_BLOCKS = (5, 4, 7, 6, 3, 2, 1, 0)
+GATHER_BLOCKS = (3, 1, 7, 5, 0, 2, 6, 4)
 
 
 def groups(planes, blocks):
@@ -21,13 +25,11 @@
     for p in range(pairs):
         swapped = (p % half == half // 4) != (p >= half)
         plane.append([2 * p + (m ^ swapped) for m in range(2)])
-    alternate = [b for start in (0, blocks // 2) for b in range(start, start + blocks // 2)]
-    alternate = [alternate[(i % 2) * (blocks // 2) + i // 2] for i in range(blocks)]
-    cores = [b for core in range(2) for b in alternate if b % 2 == core]
-    near = [[plane[p][m] * blocks + b for b in cores for m in range(2)] for p in range(pairs)]
+    near = [[plane[p][m] * blocks + b for b in NEAR_BLOCKS for m in range(2)] for p in range(pairs)]
+    gather = [[plane[p][m] * blocks + b for b in GATHER_BLOCKS for m in range(2)] for p in range(pairs)]
     order = [*range(half, pairs), *reversed(range(half))]
     far = [[plane[p][m] for p in order] for m in range(2)]
-    return near, far
+    return near, far, gather
 
 
 def exchange(x, axes, axis_groups=None):
@@ -168,16 +170,21 @@
     picked[...] = stats
 
 
-def scale_kernel(floor, gathered, total, out, buf, sems):
-    factor = jnp.sqrt(jnp.maximum(total[...], floor))[:, out.shape[2] - 1 :]
-    pieces = sems.shape[0]
-    size = gathered.shape[0] // pieces
-    copies = []
-    for i in range(pieces):
-        part = slice(i * size, (i + 1) * size)
-        buf[part] = gathered[part] * factor[None]
-        copies.append(pltpu.make_async_copy(buf.at[part], out.at[part], sems.at[i]))
-        copies[-1].start()
+def scale_kernel(places, floor, gathered, total, out, buf, sems):
+    total = jnp.sum(total[...], axis=0, keepdims=True)
+    factor = jnp.sqrt(jnp.maximum(total, floor))[:, total.shape[1] - 1 :]
+    rows = gathered.shape[1]
+    for slot, place in enumerate(places):
+        buf[place * rows : (place + 1) * rows] = gathered[slot] * factor
+    size = buf.shape[0] // sems.shape[0]
+    copies = [
+        pltpu.make_async_copy(
+            buf.at[pl.ds(i * size, size)], out.at[pl.ds(i * size, size)], sems.at[i]
+        )
+        for i in range(sems.shape[0])
+    ]
+    for copy in copies:
+        copy.start()
     for copy in copies:
         copy.wait()
 
@@ -185,7 +192,7 @@
 SMALL = pltpu.CompilerParams(vmem_limit_bytes=4 << 20)
 
 
-def on_device(near_groups, far_groups, propagator, site_coords, momenta, source_slice):
+def on_device(near_groups, far_groups, gather_groups, propagator, site_coords, momenta, source_slice):
     _, sinks, sources, _, slices, local_sites = propagator.shape
     pairs = sinks * sources
     lanes = 2 * momenta.shape[1]
@@ -213,26 +220,27 @@
         out_specs=(IN_VMEM, IN_VMEM),
         compiler_params=SMALL,
     )(received.reshape(far * (rows + 1), lanes))
-    gathered = exchange(scaled, SITE_AXES, near_groups)
-    picked = lax.psum(picked, "ta")
+    gathered = exchange(scaled, SITE_AXES, gather_groups)
+    picked = lax.all_gather(picked, "ta", axis=0, tiled=True)
+    places = [near_groups[0].index(member) for member in gather_groups[0]]
     correlator = pl.pallas_call(
-        functools.partial(scale_kernel, all_sites),
-        out_shape=jax.ShapeDtypeStruct((pairs, slices, lanes), jnp.float32),
+        functools.partial(scale_kernel, places, all_sites),
+        out_shape=jax.ShapeDtypeStruct((near * rows, lanes), jnp.float32),
         in_specs=[IN_VMEM] * 2,
-        out_specs=pl.BlockSpec(memory_space=pltpu.HBM),
+        out_specs=IN_HBM,
         scratch_shapes=[
-            pltpu.VMEM((pairs, slices, lanes), jnp.float32),
+            pltpu.VMEM((near * rows, lanes), jnp.float32),
             pltpu.SemaphoreType.DMA((2,)),
         ],
         compiler_params=SMALL,
-    )(gathered.reshape(pairs, slices, lanes), picked)
-    return correlator
+    )(gathered, picked)
+    return correlator.reshape(pairs, slices, lanes)
 
 
 def solution(mesh):
-    near_groups, far_groups = groups(mesh.shape["xy"], mesh.shape["gz"])
+    near_groups, far_groups, gather_groups = groups(mesh.shape["xy"], mesh.shape["gz"])
     return jax.shard_map(
-        functools.partial(on_device, near_groups, far_groups),
+        functools.partial(on_device, near_groups, far_groups, gather_groups),
         mesh=mesh,
         in_specs=(P(None, None, None, None, "ta", SITE_AXES), P(None, SITE_AXES), P(), P()),
         out_specs=P(None, "ta", None),

time: 55.6 us -> 53.7 us (0.966)
  blocking collectives: 44.4 us -> 43.5 us
  starting transfers between devices: 5.68 us -> 5.06 us
    psum x1 -> x0, blocking collectives: 8.75 us -> none  [on_device(): picked = lax.psum(picked, 'ta')]
    all_gather x0 -> x1, blocking collectives: none -> 7.99 us  [on_device(): picked = lax.all_gather(picked, 'ta', axis=0, tiled=True)]
    all_to_all x1, starting transfers between devices: 5.68 us -> 5.06 us  [exchange(): lax.all_to_all(x, axes, split_axis=0, concat_axis=0, tiled=True, axis_ind...]
where the time goes in v6:
time: 53.7 us; the launch traced here: 53.1 us
  blocking collectives  43.5 us (81%)
  starting transfers between devices  5.06 us (9%)
  Pallas kernels  4.5 us (8%)
    all_to_all x2, blocking collectives, exchange(): lax.all_to_all(x, axes, split_axis=0, concat_axis=0, tiled=True, axis_ind...  35.5 us
    all_gather x1, blocking collectives, on_device(): picked = lax.all_gather(picked, 'ta', axis=0, tiled=True)  7.99 us
    all_to_all x1, starting transfers between devices, exchange(): lax.all_to_all(x, axes, split_axis=0, concat_axis=0, tiled=True, axis_ind...  5.06 us
    pallas_call x1, Pallas kernels, project(): pl.pallas_call(functools.partial(project_kernel, near), out_shape=jax.Sha...  2.84 us
  transfers between devices with their start and end apart: 1, of which 0 were waited for; matrix products, arithmetic and copies ran while one was open for 0% of the time, Pallas kernels for 0%

profile of v6, /device:TPU:1, one launch (start us, length us, event | category | flops | bytes accessed | tf_op | source)
XLA Modules:
  0.0 53.1 jit_solution(16895161862660098391)
XLA Ops:
  0.0 2.8 %shard_map.46 = f32[528,128]{1,0:T(8,128)S(1)} custom-call(f32[2,4,4,9,32,128]{5,4,3,2,1,0:T(8,128)} %propagator.1, s32[3,128]{1,0:T(4,128)} %coords.1, s32[3,64]{1,0:T(4,128)} %momenta.1, s32[4]{0:T(128)} %source.1), custom_call_target="tpu_custom_call" | custom-call | tf_op jit(solution)/shard_map/pallas_call | solution.py:124
  2.8 15.9 %all_to_all.15 = f32[16,33,1,128]{3,2,1,0:T(1,128)S(1)} all-to-all(f32[16,33,1,128]{3,2,1,0:T(1,128)S(1)} %bitcast.7), channel_id=1, replica_groups={{5,13,4,12,7,15,6,14,3,11,2,10,1,9,0,8},{29,21,28,20,31,23,30,22,27,19,..., dimensions={0} | all-to-all | bytes 540672 | tf_op jit(solution)/shard_map/all_to_all | solution.py:36
  18.8 19.6 %all_to_all.16 = f32[8,33,1,128]{3,2,1,0:T(1,128)S(1)} all-to-all(f32[8,33,1,128]{3,2,1,0:T(1,128)S(1)} %bitcast.9), channel_id=1, replica_groups={{72,80,104,120,48,32,24,0},{64,88,96,112,56,40,16,8},{73,81,105,121,49,..., dimensions={0} | all-to-all | bytes 270336 | tf_op jit(solution)/shard_map/all_to_all | solution.py:36
  38.4 0.8 %shard_map.48 = (f32[16,32,128]{2,1,0:T(8,128)}, f32[1,128]{1,0:T(1,128)S(1)}) custom-call(f32[264,128]{1,0:T(8,128)S(1)} %bitcast.10), custom_call_target="tpu_custom_call" | custom-call | tf_op jit(solution)/shard_map/pallas_call | solution.py:213
  39.2 5.1 %all-to-all-start.2 = ((f32[16,32,128]{2,1,0:T(8,128)}), f32[16,32,128]{2,1,0:T(8,128)S(1)}, u32[]{:S(2)}, u32[]{:S(2)}) async-start(f32[16,32,128]{2,1,0:T(8,128)} %get-tuple-element.7), calls=%async_computation.2 | async-start | bytes 524288 | tf_op jit(solution)/shard_map/all_to_all | solution.py:36
  44.3 8.0 %all-gather = f32[4,1,128]{2,1,0:T(1,128)S(1)} all-gather(f32[1,1,128]{2,1,0:T(1,128)S(1)} %bitcast.12), channel_id=1, replica_groups=mesh['ta'=4,'xy'=16,'gz'=8] {'ta'}, dimensions={0}, use_global_device_ids=true | all-gather | bytes 2560 | tf_op jit(solution)/shard_map/all_gather | solution.py:224
  52.3 0.0 all-to-all-done.2.gathered
  52.3 0.8 %shard_map.49 = f32[512,128]{1,0:T(8,128)} custom-call(f32[16,32,128]{2,1,0:T(8,128)S(1)} %all-to-all-done.2.gathered, f32[4,128]{1,0:T(4,128)S(1)} %bitcast.11), custom_call_target="tpu_custom_call" | custom-call | tf_op jit(solution)/shard_map/pallas_call | solution.py:226
  (1 shorter events, 0.0 us)
Async XLA Ops:
  39.2 13.0 %all-to-all-start.2 = ((f32[16,32,128]{2,1,0:T(8,128)}), f32[16,32,128]{2,1,0:T(8,128)S(1)}, u32[]{:S(2)}, u32[]{:S(2)}) async-start(f32[16,32,128]{2,1,0:T(8,128)} %get-tuple-element.7), calls=%async_computation.2 | async-start | bytes 524288 | tf_op jit(solution)/shard_map/all_to_all | solution.py:36

commit v7 on v6

--- a/solution.py
+++ b/solution.py
@@ -221,7 +221,13 @@
         compiler_params=SMALL,
     )(received.reshape(far * (rows + 1), lanes))
     gathered = exchange(scaled, SITE_AXES, gather_groups)
-    picked = lax.all_gather(picked, "ta", axis=0, tiled=True)
+    picked = lax.all_gather(
+        picked,
+        "ta",
+        axis=0,
+        tiled=True,
+        axis_index_groups=[[*reversed(range(lax.axis_size("ta")))]],
+    )
     places = [near_groups[0].index(member) for member in gather_groups[0]]
     correlator = pl.pallas_call(
         functools.partial(scale_kernel, places, all_sites),

time: 53.7 us -> 52.5 us (0.978)
  blocking collectives: 43.5 us -> 42.6 us
    all_gather x1, blocking collectives: 7.99 us -> 7.07 us  [on_device(): lax.all_gather(picked, 'ta', axis=0, tiled=True, axis_index_groups=[[*rev...]
where the time goes in v7:
time: 52.5 us; the launch traced here: 52.2 us
  blocking collectives  42.6 us (81%)
  starting transfers between devices  5.06 us (10%)
  Pallas kernels  4.5 us (9%)
    all_to_all x2, blocking collectives, exchange(): lax.all_to_all(x, axes, split_axis=0, concat_axis=0, tiled=True, axis_ind...  35.5 us
    all_gather x1, blocking collectives, on_device(): lax.all_gather(picked, 'ta', axis=0, tiled=True, axis_index_groups=[[*rev...  7.07 us
    all_to_all x1, starting transfers between devices, exchange(): lax.all_to_all(x, axes, split_axis=0, concat_axis=0, tiled=True, axis_ind...  5.06 us
    pallas_call x1, Pallas kernels, project(): pl.pallas_call(functools.partial(project_kernel, near), out_shape=jax.Sha...  2.84 us
  transfers between devices with their start and end apart: 1, of which 0 were waited for; matrix products, arithmetic and copies ran while one was open for 0% of the time, Pallas kernels for 0%

profile of v7, /device:TPU:1, one launch (start us, length us, event | category | flops | bytes accessed | tf_op | source)
XLA Modules:
  0.0 52.2 jit_solution(6386182724091712518)
XLA Ops:
  0.0 2.8 %shard_map.46 = f32[528,128]{1,0:T(8,128)S(1)} custom-call(f32[2,4,4,9,32,128]{5,4,3,2,1,0:T(8,128)} %propagator.1, s32[3,128]{1,0:T(4,128)} %coords.1, s32[3,64]{1,0:T(4,128)} %momenta.1, s32[4]{0:T(128)} %source.1), custom_call_target="tpu_custom_call" | custom-call | tf_op jit(solution)/shard_map/pallas_call | solution.py:124
  2.8 15.9 %all_to_all.15 = f32[16,33,1,128]{3,2,1,0:T(1,128)S(1)} all-to-all(f32[16,33,1,128]{3,2,1,0:T(1,128)S(1)} %bitcast.7), channel_id=1, replica_groups={{5,13,4,12,7,15,6,14,3,11,2,10,1,9,0,8},{29,21,28,20,31,23,30,22,27,19,..., dimensions={0} | all-to-all | bytes 540672 | tf_op jit(solution)/shard_map/all_to_all | solution.py:36
  18.8 19.6 %all_to_all.16 = f32[8,33,1,128]{3,2,1,0:T(1,128)S(1)} all-to-all(f32[8,33,1,128]{3,2,1,0:T(1,128)S(1)} %bitcast.9), channel_id=1, replica_groups={{72,80,104,120,48,32,24,0},{64,88,96,112,56,40,16,8},{73,81,105,121,49,..., dimensions={0} | all-to-all | bytes 270336 | tf_op jit(solution)/shard_map/all_to_all | solution.py:36
  38.4 0.8 %shard_map.48 = (f32[16,32,128]{2,1,0:T(8,128)}, f32[1,128]{1,0:T(1,128)S(1)}) custom-call(f32[264,128]{1,0:T(8,128)S(1)} %bitcast.10), custom_call_target="tpu_custom_call" | custom-call | tf_op jit(solution)/shard_map/pallas_call | solution.py:213
  39.2 5.1 %all-to-all-start.2 = ((f32[16,32,128]{2,1,0:T(8,128)}), f32[16,32,128]{2,1,0:T(8,128)S(1)}, u32[]{:S(2)}, u32[]{:S(2)}) async-start(f32[16,32,128]{2,1,0:T(8,128)} %get-tuple-element.7), calls=%async_computation.2 | async-start | bytes 524288 | tf_op jit(solution)/shard_map/all_to_all | solution.py:36
  44.3 7.1 %all-gather = f32[4,1,128]{2,1,0:T(1,128)S(1)} all-gather(f32[1,1,128]{2,1,0:T(1,128)S(1)} %bitcast.12), channel_id=1, replica_groups={{384,256,128,0},{385,257,129,1},{386,258,130,2},{387,259,131,3},{388,26..., dimensions={0}, use_global_device_ids=true | all-gather | bytes 2560 | tf_op jit(solution)/shard_map/all_gather | solution.py:224
  51.4 0.0 all-to-all-done.2.gathered
  51.4 0.8 %shard_map.49 = f32[512,128]{1,0:T(8,128)} custom-call(f32[16,32,128]{2,1,0:T(8,128)S(1)} %all-to-all-done.2.gathered, f32[4,128]{1,0:T(4,128)S(1)} %bitcast.11), custom_call_target="tpu_custom_call" | custom-call | tf_op jit(solution)/shard_map/pallas_call | solution.py:232
  (1 shorter events, 0.0 us)
Async XLA Ops:
  39.2 12.1 %all-to-all-start.2 = ((f32[16,32,128]{2,1,0:T(8,128)}), f32[16,32,128]{2,1,0:T(8,128)S(1)}, u32[]{:S(2)}, u32[]{:S(2)}) async-start(f32[16,32,128]{2,1,0:T(8,128)} %get-tuple-element.7), calls=%async_computation.2 | async-start | bytes 524288 | tf_op jit(solution)/shard_map/all_to_all | solution.py:36

commit v8 on v7

--- a/solution.py
+++ b/solution.py
@@ -15,7 +15,7 @@
 
 
 NEAR_BLOCKS = (5, 4, 7, 6, 3, 2, 1, 0)
-GATHER_BLOCKS = (3, 1, 7, 5, 0, 2, 6, 4)
+GATHER_BLOCKS = (3, 2, 1, 0, 5, 4, 7, 6)
 
 
 def groups(planes, blocks):
@@ -27,7 +27,8 @@
         plane.append([2 * p + (m ^ swapped) for m in range(2)])
     near = [[plane[p][m] * blocks + b for b in NEAR_BLOCKS for m in range(2)] for p in range(pairs)]
     gather = [[plane[p][m] * blocks + b for b in GATHER_BLOCKS for m in range(2)] for p in range(pairs)]
-    order = [*range(half, pairs), *reversed(range(half))]
+    late = half + 1
+    order = [late, *(p for p in reversed(range(pairs)) if p != late)]
     far = [[plane[p][m] for p in order] for m in range(2)]
     return near, far, gather
 
@@ -226,7 +227,7 @@
         "ta",
         axis=0,
         tiled=True,
-        axis_index_groups=[[*reversed(range(lax.axis_size("ta")))]],
+        axis_index_groups=[[(1 - t) % lax.axis_size("ta") for t in range(lax.axis_size("ta"))]],
     )
     places = [near_groups[0].index(member) for member in gather_groups[0]]
     correlator = pl.pallas_call(

time: 52.5 us -> 52.2 us (level)
  blocking collectives: 42.6 us -> 39.8 us
  starting transfers between devices: 5.06 us -> 7.26 us
    all_to_all x2, blocking collectives: 35.5 us -> 33.1 us  [exchange(): lax.all_to_all(x, axes, split_axis=0, concat_axis=0, tiled=True, axis_ind...]
    all_to_all x1, starting transfers between devices: 5.06 us -> 7.26 us  [exchange(): lax.all_to_all(x, axes, split_axis=0, concat_axis=0, tiled=True, axis_ind...]
where the time goes in v8:
time: 52.2 us; the launch traced here: 51.6 us
  blocking collectives  39.8 us (76%)
  starting transfers between devices  7.26 us (14%)
  Pallas kernels  4.5 us (9%)
    all_to_all x2, blocking collectives, exchange(): lax.all_to_all(x, axes, split_axis=0, concat_axis=0, tiled=True, axis_ind...  33.1 us
    all_to_all x1, starting transfers between devices, exchange(): lax.all_to_all(x, axes, split_axis=0, concat_axis=0, tiled=True, axis_ind...  7.26 us
    all_gather x1, blocking collectives, on_device(): lax.all_gather(picked, 'ta', axis=0, tiled=True, axis_index_groups=[[(1 -...  6.78 us
    pallas_call x1, Pallas kernels, project(): pl.pallas_call(functools.partial(project_kernel, near), out_shape=jax.Sha...  2.84 us
  transfers between devices with their start and end apart: 1, of which 0 were waited for; matrix products, arithmetic and copies ran while one was open for 0% of the time, Pallas kernels for 0%

profile of v8, /device:TPU:1, one launch (start us, length us, event | category | flops | bytes accessed | tf_op | source)
XLA Modules:
  0.0 51.6 jit_solution(11794012406419333195)
XLA Ops:
  0.0 2.8 %shard_map.46 = f32[528,128]{1,0:T(8,128)S(1)} custom-call(f32[2,4,4,9,32,128]{5,4,3,2,1,0:T(8,128)} %propagator.1, s32[3,128]{1,0:T(4,128)} %coords.1, s32[3,64]{1,0:T(4,128)} %momenta.1, s32[4]{0:T(128)} %source.1), custom_call_target="tpu_custom_call" | custom-call | tf_op jit(solution)/shard_map/pallas_call | solution.py:125
  2.8 15.9 %all_to_all.15 = f32[16,33,1,128]{3,2,1,0:T(1,128)S(1)} all-to-all(f32[16,33,1,128]{3,2,1,0:T(1,128)S(1)} %bitcast.7), channel_id=1, replica_groups={{5,13,4,12,7,15,6,14,3,11,2,10,1,9,0,8},{29,21,28,20,31,23,30,22,27,19,..., dimensions={0} | all-to-all | bytes 540672 | tf_op jit(solution)/shard_map/all_to_all | solution.py:37
  18.8 17.1 %all_to_all.16 = f32[8,33,1,128]{3,2,1,0:T(1,128)S(1)} all-to-all(f32[8,33,1,128]{3,2,1,0:T(1,128)S(1)} %bitcast.9), channel_id=1, replica_groups={{80,120,104,72,48,32,24,0},{88,112,96,64,56,40,16,8},{81,121,105,73,49,..., dimensions={0} | all-to-all | bytes 270336 | tf_op jit(solution)/shard_map/all_to_all | solution.py:37
  35.9 0.8 %shard_map.48 = (f32[16,32,128]{2,1,0:T(8,128)}, f32[1,128]{1,0:T(1,128)S(1)}) custom-call(f32[264,128]{1,0:T(8,128)S(1)} %bitcast.10), custom_call_target="tpu_custom_call" | custom-call | tf_op jit(solution)/shard_map/pallas_call | solution.py:214
  36.8 7.3 %all-to-all-start.2 = ((f32[16,32,128]{2,1,0:T(8,128)}), f32[16,32,128]{2,1,0:T(8,128)S(1)}, u32[]{:S(2)}, u32[]{:S(2)}) async-start(f32[16,32,128]{2,1,0:T(8,128)} %get-tuple-element.7), calls=%async_computation.2 | async-start | bytes 524288 | tf_op jit(solution)/shard_map/all_to_all | solution.py:37
  44.0 6.8 %all-gather = f32[4,1,128]{2,1,0:T(1,128)S(1)} all-gather(f32[1,1,128]{2,1,0:T(1,128)S(1)} %bitcast.12), channel_id=1, replica_groups={{128,0,384,256},{129,1,385,257},{130,2,386,258},{131,3,387,259},{132,4,..., dimensions={0}, use_global_device_ids=true | all-gather | bytes 2560 | tf_op jit(solution)/shard_map/all_gather | solution.py:225
  50.8 0.0 all-to-all-done.2.gathered
  50.8 0.8 %shard_map.49 = f32[512,128]{1,0:T(8,128)} custom-call(f32[16,32,128]{2,1,0:T(8,128)S(1)} %all-to-all-done.2.gathered, f32[4,128]{1,0:T(4,128)S(1)} %bitcast.11), custom_call_target="tpu_custom_call" | custom-call | tf_op jit(solution)/shard_map/pallas_call | solution.py:233
  (1 shorter events, 0.0 us)
Async XLA Ops:
  36.8 14.0 %all-to-all-start.2 = ((f32[16,32,128]{2,1,0:T(8,128)}), f32[16,32,128]{2,1,0:T(8,128)S(1)}, u32[]{:S(2)}, u32[]{:S(2)}) async-start(f32[16,32,128]{2,1,0:T(8,128)} %get-tuple-element.7), calls=%async_computation.2 | async-start | bytes 524288 | tf_op jit(solution)/shard_map/all_to_all | solution.py:37

commit v9 on v8

--- a/solution.py
+++ b/solution.py
@@ -175,17 +175,16 @@
     total = jnp.sum(total[...], axis=0, keepdims=True)
     factor = jnp.sqrt(jnp.maximum(total, floor))[:, total.shape[1] - 1 :]
     rows = gathered.shape[1]
-    for slot, place in enumerate(places):
-        buf[place * rows : (place + 1) * rows] = gathered[slot] * factor
     size = buf.shape[0] // sems.shape[0]
-    copies = [
-        pltpu.make_async_copy(
-            buf.at[pl.ds(i * size, size)], out.at[pl.ds(i * size, size)], sems.at[i]
-        )
-        for i in range(sems.shape[0])
-    ]
-    for copy in copies:
-        copy.start()
+    copies = []
+    for place in range(len(places)):
+        buf[place * rows : (place + 1) * rows] = gathered[places.index(place)] * factor
+        if (place + 1) * rows % size == 0:
+            part = pl.ds(len(copies) * size, size)
+            copies.append(
+                pltpu.make_async_copy(buf.at[part], out.at[part], sems.at[len(copies)])
+            )
+            copies[-1].start()
     for copy in copies:
         copy.wait()
 
@@ -237,7 +236,7 @@
         out_specs=IN_HBM,
         scratch_shapes=[
             pltpu.VMEM((near * rows, lanes), jnp.float32),
-            pltpu.SemaphoreType.DMA((2,)),
+            pltpu.SemaphoreType.DMA((4,)),
         ],
         compiler_params=SMALL,
     )(gathered, picked)

time: 52.2 us -> 52.2 us (level)
  no operation moved by 1% of the time
where the time goes in v9:
time: 52.2 us; the launch traced here: 51.6 us
  blocking collectives  39.8 us (76%)
  starting transfers between devices  7.26 us (14%)
  Pallas kernels  4.5 us (9%)
    all_to_all x2, blocking collectives, exchange(): lax.all_to_all(x, axes, split_axis=0, concat_axis=0, tiled=True, axis_ind...  33.1 us
    all_to_all x1, starting transfers between devices, exchange(): lax.all_to_all(x, axes, split_axis=0, concat_axis=0, tiled=True, axis_ind...  7.26 us
    all_gather x1, blocking collectives, on_device(): lax.all_gather(picked, 'ta', axis=0, tiled=True, axis_index_groups=[[(1 -...  6.78 us
    pallas_call x1, Pallas kernels, project(): pl.pallas_call(functools.partial(project_kernel, near), out_shape=jax.Sha...  2.84 us
  transfers between devices with their start and end apart: 1, of which 0 were waited for; matrix products, arithmetic and copies ran while one was open for 0% of the time, Pallas kernels for 0%

profile of v9, /device:TPU:1, one launch (start us, length us, event | category | flops | bytes accessed | tf_op | source)
XLA Modules:
  0.0 51.6 jit_solution(5464288199381663696)
XLA Ops:
  0.0 2.8 %shard_map.46 = f32[528,128]{1,0:T(8,128)S(1)} custom-call(f32[2,4,4,9,32,128]{5,4,3,2,1,0:T(8,128)} %propagator.1, s32[3,128]{1,0:T(4,128)} %coords.1, s32[3,64]{1,0:T(4,128)} %momenta.1, s32[4]{0:T(128)} %source.1), custom_call_target="tpu_custom_call" | custom-call | tf_op jit(solution)/shard_map/pallas_call | solution.py:125
  2.8 15.9 %all_to_all.15 = f32[16,33,1,128]{3,2,1,0:T(1,128)S(1)} all-to-all(f32[16,33,1,128]{3,2,1,0:T(1,128)S(1)} %bitcast.7), channel_id=1, replica_groups={{5,13,4,12,7,15,6,14,3,11,2,10,1,9,0,8},{29,21,28,20,31,23,30,22,27,19,..., dimensions={0} | all-to-all | bytes 540672 | tf_op jit(solution)/shard_map/all_to_all | solution.py:37
  18.8 17.1 %all_to_all.16 = f32[8,33,1,128]{3,2,1,0:T(1,128)S(1)} all-to-all(f32[8,33,1,128]{3,2,1,0:T(1,128)S(1)} %bitcast.9), channel_id=1, replica_groups={{80,120,104,72,48,32,24,0},{88,112,96,64,56,40,16,8},{81,121,105,73,49,..., dimensions={0} | all-to-all | bytes 270336 | tf_op jit(solution)/shard_map/all_to_all | solution.py:37
  35.9 0.8 %shard_map.48 = (f32[16,32,128]{2,1,0:T(8,128)}, f32[1,128]{1,0:T(1,128)S(1)}) custom-call(f32[264,128]{1,0:T(8,128)S(1)} %bitcast.10), custom_call_target="tpu_custom_call" | custom-call | tf_op jit(solution)/shard_map/pallas_call | solution.py:213
  36.8 7.3 %all-to-all-start.2 = ((f32[16,32,128]{2,1,0:T(8,128)}), f32[16,32,128]{2,1,0:T(8,128)S(1)}, u32[]{:S(2)}, u32[]{:S(2)}) async-start(f32[16,32,128]{2,1,0:T(8,128)} %get-tuple-element.7), calls=%async_computation.2 | async-start | bytes 524288 | tf_op jit(solution)/shard_map/all_to_all | solution.py:37
  44.0 6.8 %all-gather = f32[4,1,128]{2,1,0:T(1,128)S(1)} all-gather(f32[1,1,128]{2,1,0:T(1,128)S(1)} %bitcast.12), channel_id=1, replica_groups={{128,0,384,256},{129,1,385,257},{130,2,386,258},{131,3,387,259},{132,4,..., dimensions={0}, use_global_device_ids=true | all-gather | bytes 2560 | tf_op jit(solution)/shard_map/all_gather | solution.py:224
  50.8 0.0 all-to-all-done.2.gathered
  50.8 0.8 %shard_map.49 = f32[512,128]{1,0:T(8,128)} custom-call(f32[16,32,128]{2,1,0:T(8,128)S(1)} %all-to-all-done.2.gathered, f32[4,128]{1,0:T(4,128)S(1)} %bitcast.11), custom_call_target="tpu_custom_call" | custom-call | tf_op jit(solution)/shard_map/pallas_call | solution.py:232
  (1 shorter events, 0.0 us)
Async XLA Ops:
  36.8 14.0 %all-to-all-start.2 = ((f32[16,32,128]{2,1,0:T(8,128)}), f32[16,32,128]{2,1,0:T(8,128)S(1)}, u32[]{:S(2)}, u32[]{:S(2)}) async-start(f32[16,32,128]{2,1,0:T(8,128)} %get-tuple-element.7), calls=%async_computation.2 | async-start | bytes 524288 | tf_op jit(solution)/shard_map/all_to_all | solution.py:37
